TPU v7x, 512 devices: a 4x2x32 block of a 4x8x32 slice. The times are simulated.
512 devices in a mesh: parts: 2 (over y), blk: 128 (over z, x), merge: 2 (over core).
Axes of the slice: x: 4, y: 2, z: 32, core: 2. Of those that a mesh axis runs over, the one named last changes fastest.
The devices are a block of a 4x8x32 slice.
Arguments:
- queries: bfloat16 [2048, 1024], P('blk'), may hold values from -102 to 102
- spans: bfloat16 [65536, 1024], P(('parts', 'blk', 'merge')), parts along dimension 0, may hold values from -0.5 to 0.5
- span_doc: int32 [65536], P(('parts', 'blk', 'merge')), parts along dimension 0, may hold values from 0 to 127
- span_valid: int32 [65536], P(('parts', 'blk', 'merge')), parts along dimension 0, may hold values 0 or 1
- doc_bias: float32 [128], replicated, may hold values from -3 to 0
Outputs:
- soft_match: float32 [4096], P(('parts', 'blk')), parts along dimension 0
- top_score: float32 [4096], P(('parts', 'blk')), parts along dimension 0
There are 2 independent parts, one for each index of `parts`. A program takes and returns all parts, laid end to end along the dimension named above; an argument that names none is the same for every part. Nothing has to cross between parts.
All inputs are finite; a program needn't handle non-finite values. No bound on the sum of `span_valid` on one device may be relied on, other than what follows from the above.
Results may differ from a plain program's by a relative error of at most 0.0003.
Values may be sent and summed in bfloat16 or wider, within the bound.
No kernel may reach another device: no remote copies, remote signals or barrier semaphores. Data moves between devices by JAX's collectives and lax.ppermute only.
A program may use at most 64 MiB of HBM per device.

v0:
```python
import jax
import jax.numpy as jnp
from jax import lax
from jax.sharding import Mesh
from jax.sharding import PartitionSpec as P

BLK = ("blk_0", "blk_1")
PARTS_BLK_MERGE = ("parts", "blk_0", "blk_1", "merge")
PARTS_BLK = ("parts", "blk_0", "blk_1")


def joined_along(parts, dim):
    dims = list(parts.shape[1:])
    dims[dim] *= parts.shape[0]
    return jnp.moveaxis(parts, 0, dim).reshape(dims)


def stacked_from(value, axes, order):
    parts = value
    for k in order:
        parts = lax.all_gather(parts, axes[k])
    done = order[::-1]
    back = [done.index(k) for k in range(len(axes))]
    parts = parts.transpose(*back, *range(len(axes), parts.ndim))
    return parts.reshape(-1, *value.shape)


def whole_of(value, axes, order, dim):
    return joined_along(stacked_from(value, axes, order), dim)


def from_everyone(value, axis):
    peers = lax.axis_size(axis)
    return lax.all_to_all(
        jnp.broadcast_to(value[None], (peers, *value.shape)), axis, 0, 0, tiled=True
    )


def all_in_one(value, axis):
    leaves = jax.tree.leaves(value)
    order = sorted(range(len(leaves)), key=lambda k: -leaves[k].size)
    width = (1, *leaves[order[0]].shape)[-1]
    lines = [
        jnp.pad(leaves[k].reshape(-1), (0, -leaves[k].size % width)).reshape(-1, width)
        for k in order
    ]
    both, at, found = (from_everyone(jnp.concatenate(lines), axis), 0, {})
    for k, line in zip(order, lines):
        piece = both[:, at : at + len(line)].reshape(len(both), -1)
        found[k] = piece[:, : leaves[k].size].reshape(-1, *leaves[k].shape)
        at += len(line)
    numbers = iter(range(len(leaves)))
    return jax.tree.map(lambda _: found[next(numbers)], value)


def folded_in_pairs(pieces, combine):
    while len(jax.tree.leaves(pieces)[0]) > 1:
        pieces = jax.vmap(combine)(
            *(jax.tree.map(lambda part: part[side::2], pieces) for side in (0, 1))
        )
    return jax.tree.map(lambda part: part[0], pieces)


def joined_all(value, axis, combine):
    pieces = all_in_one(value, axis)
    return folded_in_pairs(pieces, combine)


def span_bias(span_doc, doc_bias):
    onehot = span_doc[:, None] == jnp.arange(doc_bias.shape[0], dtype=jnp.int32)[None, :]
    return jnp.sum(jnp.where(onehot, doc_bias[None, :], jnp.zeros_like(doc_bias)[None, :]), axis=1)


def block_stats(rows, spans, bias, valid):
    similarity = lax.dot_general(
        rows, spans, (((1,), (1,)), ((), ())), preferred_element_type=jnp.float32
    )
    logit = jnp.where(valid[None, :], 2.0 * similarity + bias[None, :], -jnp.inf)
    highest = jnp.max(logit, axis=1)
    total = jnp.sum(jnp.exp(logit - highest[:, None]), axis=1)
    best = jnp.max(jnp.where(valid[None, :], similarity, -jnp.inf), axis=1)
    return (highest, total, best)


def stats_in_blocks(rows, spans, bias, valid):
    length = rows.shape[0]
    grouped = rows.reshape(length // 512, 512, rows.shape[1])
    results = lax.map(lambda piece: jnp.stack(block_stats(piece, spans, bias, valid)), grouped)
    return jnp.transpose(results, (1, 0, 2)).reshape(3, length)


def join_triples(first, second):
    highest = jnp.maximum(first[0], second[0])
    total = first[1] * jnp.exp(first[0] - highest) + second[1] * jnp.exp(second[0] - highest)
    return (highest, total, jnp.maximum(first[2], second[2]))


def shards(queries, spans, span_doc, span_valid, doc_bias):
    bias = span_bias(span_doc, doc_bias)
    valid = span_valid == 1
    stacked = stats_in_blocks(whole_of(queries, BLK, (0, 1), 0), spans, bias, valid)
    highest, total, best = (stacked[0], stacked[1], stacked[2])
    high_rows, total_rows, best_rows = (
        lax.all_to_all(highest[None, :], BLK, split_axis=1, concat_axis=0, tiled=True),
        lax.all_to_all(total[None, :], BLK, split_axis=1, concat_axis=0, tiled=True),
        lax.all_to_all(best[None, :], BLK, split_axis=1, concat_axis=0, tiled=True),
    )
    local_top = jnp.max(high_rows, axis=0)
    local_total = jnp.sum(total_rows * jnp.exp(high_rows - local_top[None, :]), axis=0)
    local_best = jnp.max(best_rows, axis=0)
    own_top, share, own_best = joined_all(
        (local_top, local_total, local_best), "merge", join_triples
    )
    return (own_top + jnp.log(share), own_best)


def solution(mesh):
    split = Mesh(
        mesh.devices.reshape(mesh.shape["parts"], 32, 4, mesh.shape["merge"]),
        ("parts", "blk_0", "blk_1", "merge"),
    )
    return jax.shard_map(
        shards,
        mesh=split,
        in_specs=(
            P(BLK, None),
            P(PARTS_BLK_MERGE, None),
            P(PARTS_BLK_MERGE),
            P(PARTS_BLK_MERGE),
            P(),
        ),
        out_specs=(P(PARTS_BLK), P(PARTS_BLK)),
        check_vma=False,
    )
```

profile of v0, /device:TPU:33, one launch (start us, length us, event | category | flops | bytes accessed | tf_op | source)
XLA Modules:
  0.0 370.3 jit_solution(11227095616958440813)
XLA Ops:
  7.2 0.1 all-gather.5.cloned.1.call-start
  7.2 0.7 all-gather.5.cloned.1.call-update
  8.0 0.1 all-gather.7.cloned.1.call-start
  8.0 141.3 %all-gather.5.cloned.1.call-done = bf16[512,1024]{1,0:T(8,128)(2,1)} async-done(((bf16[16,1024]{1,0:T(8,128)(2,1)}), bf16[512,1024]{1,0:T(8,128)(2,1)}) %all-gather.5.cloned.1.call-update) | async-done | bytes 1048592 | tf_op jit(solution)/shard_map/all_gather | solution.py:21
  149.4 0.8 select_reduce_fusion.1
  150.3 0.7 broadcast_compare_fusion
  150.9 77.1 %all-gather.7.cloned.1.call-done = bf16[128,16,1024]{2,1,0:T(8,128)(2,1)} async-done(((bf16[32,16,1024]{2,1,0:T(8,128)(2,1)}), bf16[128,16,1024]{2,1,0:T(8,128)(2,1)}) %all-gather.7.cloned.1.call-update) | async-done | bytes 4194320 | tf_op jit(solution)/shard_map/all_gather | solution.py:21
  228.1 5.0 %copy.12 = bf16[32,4,16,1024]{3,2,1,0:T(8,128)(2,1)} copy(bf16[32,4,16,1024]{3,2,0,1:T(8,128)(2,1)} %bitcast.66) | data formatting | bytes 8388608 | tf_op jit(solution)/shard_map/transpose | solution.py:24
  233.1 7.8 %while.10 = (s32[]{:T(128)}, f32[4,3,512]{2,1,0:T(4,128)S(1)}, pred[128]{0:T(512)(128)(4,1)S(1)}, bf16[4,512,1024]{2,1,0:T(8,128)(2,1)}, bf16[128,1024]{1,0:T(8,128)(2,1)S(1)}, /*index=5*/f32[128]{0:T(128)S(1)}, s32[]{:T(128)}) while((s32[]{:T(128)}, f32[4,3,512]{2,1,0:T(4,128)S(1)}, pred[128]{0:T(512)(128)(4,1)S(1)}, ...), condition=%wide.region_5.6_spmd, body=%wide.region_1.5_spmd.sunk | while | flops 134940160 | bytes 1859409 | solution.py:88
  233.1 1.7 fusion.16
  234.8 0.2 exponential_reduce_fusion.2
  235.0 1.7 fusion.16
  236.8 0.2 exponential_reduce_fusion.2
  237.0 1.7 fusion.16
  238.7 0.2 exponential_reduce_fusion.2
  238.9 1.7 fusion.16
  240.7 0.2 exponential_reduce_fusion.2
  240.9 0.1 slice_reduce_fusion.2
  240.9 0.7 all_to_all.37
  241.6 29.4 %all-to-all-start = ((f32[1,128,16]{2,0,1:T(1,128)}), f32[1,128,16]{2,0,1:T(1,128)S(1)}, u32[]{:S(2)}, u32[]{:S(2)}) async-start(f32[1,128,16]{2,0,1:T(1,128)} %bitcast.10), calls=%async_computation | async-start | bytes 131072 | tf_op jit(solution)/shard_map/all_to_all | solution.py:104
  271.0 0.7 all_to_all.39
  271.7 19.7 %all-to-all-done = f32[1,128,16]{2,0,1:T(1,128)S(1)} async-done(((f32[1,128,16]{2,0,1:T(1,128)}), f32[1,128,16]{2,0,1:T(1,128)S(1)}, u32[]{:S(2)}, u32[]{:S(2)}) %all-to-all-start) | async-done | bytes 8224 | tf_op jit(solution)/shard_map/all_to_all | solution.py:104
  291.4 11.5 %all-to-all-start.1 = ((f32[1,128,16]{2,0,1:T(1,128)}), f32[1,128,16]{2,0,1:T(1,128)S(1)}, u32[]{:S(2)}, u32[]{:S(2)}) async-start(f32[1,128,16]{2,0,1:T(1,128)} %bitcast.12), calls=%async_computation.1 | async-start | bytes 131072 | tf_op jit(solution)/shard_map/all_to_all | solution.py:105
  302.9 0.7 all_to_all.43
  303.6 0.2 reduce_max.36
  303.8 19.6 %all-to-all-done.1 = f32[1,128,16]{2,0,1:T(1,128)S(1)} async-done(((f32[1,128,16]{2,0,1:T(1,128)}), f32[1,128,16]{2,0,1:T(1,128)S(1)}, u32[]{:S(2)}, u32[]{:S(2)}) %all-to-all-start.1) | async-done | bytes 8224 | tf_op jit(solution)/shard_map/all_to_all | solution.py:105
  323.4 10.5 %all-to-all-start.2 = ((f32[1,128,16]{2,0,1:T(1,128)}), f32[1,128,16]{2,0,1:T(1,128)S(1)}, u32[]{:S(2)}, u32[]{:S(2)}) async-start(f32[1,128,16]{2,0,1:T(1,128)} %bitcast.16), calls=%async_computation.2 | async-start | bytes 131072 | tf_op jit(solution)/shard_map/all_to_all | solution.py:106
  333.9 20.5 %all-to-all-done.2 = f32[1,128,16]{2,0,1:T(1,128)S(1)} async-done(((f32[1,128,16]{2,0,1:T(1,128)}), f32[1,128,16]{2,0,1:T(1,128)S(1)}, u32[]{:S(2)}, u32[]{:S(2)}) %all-to-all-start.2) | async-done | bytes 8224 | tf_op jit(solution)/shard_map/all_to_all | solution.py:106
  354.4 0.2 reduce_max.37
  354.6 7.8 %all_to_all.50 = f32[2,3,16]{2,1,0:T(4,128)S(1)} all-to-all(f32[2,3,16]{2,1,0:T(4,128)S(1)} %broadcast_in_dim.56), channel_id=1, replica_groups=mesh['parts'=2,'blk_0'=32,'blk_1'=4,'merge'=2] {'merge'}, dimensions={0} | all-to-all | bytes 768 | tf_op jit(solution)/shard_map/all_to_all | solution.py:34
  362.4 0.5 fusion.6
  362.9 0.5 log_add_fusion
  (11 shorter events, 0.2 us)
Async XLA Ops:
  7.2 142.2 %all-gather.5.cloned.1.call-start = ((), (), s32[]{:S(2)}) async-start(), calls=%async_computation.4 | async-start | bytes 1081344 | tf_op jit(solution)/shard_map/all_gather | solution.py:21
  8.0 220.1 %all-gather.7.cloned.1.call-start = ((), (), s32[]{:S(2)}) async-start(), calls=%async_computation.5 | async-start | bytes 5242880 | tf_op jit(solution)/shard_map/all_gather | solution.py:21
  228.1 5.0 %copy-start = (bf16[128,1024]{1,0:T(8,128)(2,1)S(1)}, bf16[128,1024]{1,0:T(8,128)(2,1)}, u32[]{:S(2)}) copy-start(bf16[128,1024]{1,0:T(8,128)(2,1)} %param.8) | copy-start | bytes 786436
  241.6 49.7 %all-to-all-start = ((f32[1,128,16]{2,0,1:T(1,128)}), f32[1,128,16]{2,0,1:T(1,128)S(1)}, u32[]{:S(2)}, u32[]{:S(2)}) async-start(f32[1,128,16]{2,0,1:T(1,128)} %bitcast.10), calls=%async_computation | async-start | bytes 131072 | tf_op jit(solution)/shard_map/all_to_all | solution.py:104
  291.4 32.0 %all-to-all-start.1 = ((f32[1,128,16]{2,0,1:T(1,128)}), f32[1,128,16]{2,0,1:T(1,128)S(1)}, u32[]{:S(2)}, u32[]{:S(2)}) async-start(f32[1,128,16]{2,0,1:T(1,128)} %bitcast.12), calls=%async_computation.1 | async-start | bytes 131072 | tf_op jit(solution)/shard_map/all_to_all | solution.py:105
  323.4 31.0 %all-to-all-start.2 = ((f32[1,128,16]{2,0,1:T(1,128)}), f32[1,128,16]{2,0,1:T(1,128)S(1)}, u32[]{:S(2)}, u32[]{:S(2)}) async-start(f32[1,128,16]{2,0,1:T(1,128)} %bitcast.16), calls=%async_computation.2 | async-start | bytes 131072 | tf_op jit(solution)/shard_map/all_to_all | solution.py:106
Sparse Core Ops, SparseCore 0:
  10.1 139.2 all-gather.4
  151.5 76.5 all-gather.6
where the time goes:
time: 371 us; the launch traced here: 370 us
  waiting for transfers between devices  279 us (75%)
  starting transfers between devices  51.5 us (14%)
  between operations  14.1 us (4%)
  blocking collectives  7.76 us (2%)
  local copies, waits for them, and re-layouts  7.24 us (2%)
  matrix products  6.92 us (2%)
    all_gather x2, waiting for transfers between devices, stacked_from(): parts = lax.all_gather(parts, axes[k])  218 us
    all_to_all x1, starting transfers between devices, shards(): lax.all_to_all(highest[None, :], BLK, split_axis=1, concat_axis=0, tiled=...  29.4 us
    all_to_all x1, waiting for transfers between devices, shards(): lax.all_to_all(best[None, :], BLK, split_axis=1, concat_axis=0, tiled=True)  20.5 us
    all_to_all x1, waiting for transfers between devices, shards(): lax.all_to_all(highest[None, :], BLK, split_axis=1, concat_axis=0, tiled=...  19.7 us
    all_to_all x1, waiting for transfers between devices, shards(): lax.all_to_all(total[None, :], BLK, split_axis=1, concat_axis=0, tiled=True)  19.6 us
    all_to_all x1, starting transfers between devices, shards(): lax.all_to_all(total[None, :], BLK, split_axis=1, concat_axis=0, tiled=True)  11.5 us
    all_to_all x1, starting transfers between devices, shards(): lax.all_to_all(best[None, :], BLK, split_axis=1, concat_axis=0, tiled=True)  10.5 us
    all_to_all x1, blocking collectives, from_everyone(): lax.all_to_all(jnp.broadcast_to(value[None], (peers, *value.shape)), axis...  7.76 us
  transfers between devices with their start and end apart: 5, of which 5 were waited for; matrix products, arithmetic and copies ran while one was open for 0% of the time, Pallas kernels for 0%

commit v1 on v0

v1 whole, which is shorter than its diff:
```python
import jax
import jax.numpy as jnp
from jax import lax
from jax.experimental import pallas as pl
from jax.experimental.pallas import tpu as pltpu
from jax.sharding import Mesh
from jax.sharding import PartitionSpec as P

RING = 32
ROW = 4
RESIDUES = 4
LOOP = RING // RESIDUES
FIRST = RING // 2
LOW = -1e30

GROUP = ("ring", "row", "merge")


def ring_place(residue, step):
    return (FIRST + RESIDUES * step + residue) % RING


def shifted(value, axis, by):
    size = lax.axis_size(axis)
    return lax.ppermute(value, axis, [(k, (k + by) % size) for k in range(size)])


def scores_kernel(shift_ref, bias_ref, *refs):
    packs, pieces, out_ref = refs[:8], refs[8:13], refs[13]
    rows_ref, sims_ref = refs[14:]
    rows = out_ref.shape[0] // 2
    at = 0
    for piece in pieces:
        size = piece.shape[0] * piece.shape[1]
        rows_ref[at : at + size, :] = piece[...].reshape(size, piece.shape[2])
        at += size
    count = packs[0].shape[0] - 8
    docs = lax.broadcasted_iota(jnp.int32, (count, bias_ref.shape[1]), 1).astype(jnp.float32)
    best = jnp.full((1, at), LOW, jnp.float32)
    biases = []
    for k, pack in enumerate(packs):
        code = pack[count:, :128].astype(jnp.float32).T[:, :1]
        bias = jnp.sum(jnp.where(docs == code, bias_ref[...], 0.0), axis=1, keepdims=True)
        valid = code < float(bias_ref.shape[1])
        biases.append(jnp.where(valid, bias, -jnp.inf))
        sim = lax.dot_general(
            pack[:count, :], rows_ref[...], (((1,), (1,)), ((), ())), preferred_element_type=jnp.float32
        )
        sims_ref[k] = sim
        best = jnp.maximum(best, jnp.max(jnp.where(valid, sim, LOW), axis=0, keepdims=True))
    total = jnp.zeros((1, at), jnp.float32)
    for k in range(len(packs)):
        total += jnp.sum(jnp.exp(2.0 * (sims_ref[k] - best) + biases[k]), axis=0, keepdims=True)
    lane = lax.broadcasted_iota(jnp.int32, (rows, at), 1)
    line = lax.broadcasted_iota(jnp.int32, (rows, at), 0)
    per = 8 * LOOP
    slot = ((lane // per + shift_ref[0]) % RESIDUES) * LOOP + (lane // 8) % LOOP
    mine = slot == line
    query = lax.broadcasted_iota(jnp.int32, (at, 128), 0) % 8
    column = lax.broadcasted_iota(jnp.int32, (at, 128), 1)
    value = lax.dot_general(
        jnp.where(mine, best, 0.0),
        (query == column).astype(jnp.float32),
        (((1,), (0,)), ((), ())),
        precision=lax.Precision.HIGHEST,
        preferred_element_type=jnp.float32,
    ) + lax.dot_general(
        jnp.where(mine, total, 0.0),
        (query + 8 == column).astype(jnp.float32),
        (((1,), (0,)), ((), ())),
        precision=lax.Precision.HIGHEST,
        preferred_element_type=jnp.float32,
    )
    out_ref[:rows, :] = value
    out_ref[rows:, :] = value


def finish_kernel(in_ref, soft_ref, top_ref):
    rows = in_ref.shape[0] // 2
    halves = []
    for side in range(2):
        part = in_ref[side * rows : (side + 1) * rows, :]
        best = jnp.max(part, axis=0, keepdims=True)
        totals = pltpu.roll(part, 120, 1)
        total = jnp.sum(totals * jnp.exp(2.0 * jnp.minimum(part - best, 0.0)), axis=0, keepdims=True)
        halves.append((2.0 * best + jnp.log(total), best))
    first = lax.broadcasted_iota(jnp.int32, (1, 128), 1) < 8
    for out_ref, one, two in zip((soft_ref, top_ref), *halves):
        out_ref[...] = jnp.where(first, one, pltpu.roll(two, 8, 1))[:, :16]


def shards(queries, spans, span_doc, span_valid, doc_bias):
    side = lax.axis_index("merge")
    place = lax.axis_index("ring")
    half = queries.shape[0] // 2
    mine = lax.dynamic_slice_in_dim(queries, side * half, half, 0)
    code = jnp.where(span_valid == 1, span_doc, doc_bias.shape[0]).astype(jnp.bfloat16)
    codes = jnp.pad(code[None, :], ((0, 7), (0, spans.shape[1] - code.shape[0])))
    pack = jnp.concatenate([spans, codes], axis=0)

    loops = [[ring_place(r, i) for i in range(LOOP)] for r in range(RESIDUES)]
    near = lax.all_to_all(
        jnp.broadcast_to(mine[None], (LOOP, *mine.shape)), "ring", 0, 0, axis_index_groups=loops, tiled=True
    )
    row_packs = [pack, shifted(pack, "row", 1), shifted(pack, "row", -1), shifted(pack, "row", 2)]
    packs = row_packs + [shifted(one, "merge", 1) for one in row_packs]
    up = shifted(near, "ring", -1)
    down = shifted(near, "ring", 1)
    far_up = shifted(near[: LOOP // 2], "ring", -2)
    far_down = shifted(near[LOOP // 2 :], "ring", 2)

    slots = RING * 2
    stats = pl.pallas_call(
        scores_kernel,
        out_shape=jax.ShapeDtypeStruct((slots, 128), jnp.float32),
        in_specs=[pl.BlockSpec(memory_space=pltpu.SMEM)] + [pl.BlockSpec(memory_space=pltpu.VMEM)] * 14,
        out_specs=pl.BlockSpec(memory_space=pltpu.VMEM),
        scratch_shapes=[
            pltpu.VMEM((RING * half, spans.shape[1]), jnp.bfloat16),
            pltpu.VMEM((8, spans.shape[0], RING * half), jnp.float32),
        ],
        name="scores",
    )(
        (place % RESIDUES).astype(jnp.int32)[None],
        doc_bias[None, :],
        *packs,
        near,
        up,
        far_up,
        far_down,
        down,
    )
    owners = [
        (ring_place(r, i) * ROW + x) * 2 + m
        for x in range(ROW)
        for m in range(2)
        for r in range(RESIDUES)
        for i in range(LOOP)
    ]
    columns = [owners[k * slots : (k + 1) * slots] for k in range(ROW)]
    got = lax.all_to_all(stats, GROUP, 0, 0, axis_index_groups=columns, tiled=True)
    soft, top = pl.pallas_call(
        finish_kernel,
        out_shape=[jax.ShapeDtypeStruct((1, 2 * half), jnp.float32)] * 2,
        in_specs=[pl.BlockSpec(memory_space=pltpu.VMEM)],
        out_specs=[pl.BlockSpec(memory_space=pltpu.VMEM)] * 2,
        name="finish",
    )(got)
    return soft.reshape(-1), top.reshape(-1)


def solution(mesh):
    split = Mesh(
        mesh.devices.reshape(mesh.shape["parts"], RING, ROW, mesh.shape["merge"]),
        ("parts", *GROUP),
    )
    blk = ("ring", "row")
    every = ("parts", *GROUP)
    owned = P(("parts", *blk))
    return jax.shard_map(
        shards,
        mesh=split,
        in_specs=(P(blk, None), P(every, None), P(every), P(every), P()),
        out_specs=(owned, owned),
        check_vma=False,
    )
```

time: 371 us -> 137 us (0.37)
  waiting for transfers between devices: 279 us -> 2.38 us
  starting transfers between devices: 51.5 us -> 95.6 us
  blocking collectives: 7.76 us -> 29.7 us
  between operations: 14.1 us -> 1.03 us
  matrix products: 6.92 us -> 0 us
  Pallas kernels: 0 us -> 5.87 us
  local copies, waits for them, and re-layouts: 7.24 us -> 2.1 us
    all_gather x2 -> x0, waiting for transfers between devices: 218 us -> none  [stacked_from(): parts = lax.all_gather(parts, axes[k])]
    all_to_all x3 -> x1, waiting for transfers between devices: 59.8 us -> 0.01 us  [shards(): lax.all_to_all(jnp.broadcast_to(mine[None], (LOOP, *mine.shape)), 'ring',...]
    ppermute x0 -> x11, starting transfers between devices: none -> 36.8 us  [shifted(): lax.ppermute(value, axis, [(k, (k + by) % size) for k in range(size)])]
    all_to_all x1, blocking collectives: 7.76 us -> 29.7 us  [shards(): lax.all_to_all(stats, GROUP, 0, 0, axis_index_groups=columns, tiled=True)]
    all_to_all x3 -> x1, starting transfers between devices: 51.4 us -> 58.8 us  [shards(): lax.all_to_all(jnp.broadcast_to(mine[None], (LOOP, *mine.shape)), 'ring',...]
    dot_general x4 -> x0, matrix products: 6.92 us -> none  [block_stats(): lax.dot_general(rows, spans, (((1,), (1,)), ((), ())), preferred_element_...]
    pallas_call x0 -> x2, Pallas kernels: none -> 5.87 us  [the longest x1 4.45 us: shards(): pl.pallas_call(scores_kernel, out_shape=jax.ShapeDtypeStruct((slots, 128)...]
    transpose x1 -> x0, local copies, waits for them, and re-layouts: 5.04 us -> none  [stacked_from(): parts = parts.transpose(*back, *range(len(axes), parts.ndim))]
  transfers between devices with their start and end apart: 5 -> 12, of which waited for: 5 -> 1; matrix products, arithmetic and copies ran while one was open for 0% -> 0% of each run, Pallas kernels for 0% -> 0%
where the time goes in v1:
time: 137 us
  starting transfers between devices  95.6 us (70%)
  blocking collectives  29.7 us (22%)
  Pallas kernels  5.87 us (4%)
  waiting for transfers between devices  2.38 us (2%)
  local copies, waits for them, and re-layouts  2.1 us (2%)
    all_to_all x1, starting transfers between devices, shards(): lax.all_to_all(jnp.broadcast_to(mine[None], (LOOP, *mine.shape)), 'ring',...  58.8 us
    ppermute x11, starting transfers between devices, shifted(): lax.ppermute(value, axis, [(k, (k + by) % size) for k in range(size)])  36.8 us
    all_to_all x1, blocking collectives, shards(): lax.all_to_all(stats, GROUP, 0, 0, axis_index_groups=columns, tiled=True)  29.7 us
    pallas_call x1, Pallas kernels, shards(): pl.pallas_call(scores_kernel, out_shape=jax.ShapeDtypeStruct((slots, 128)...  4.45 us
  transfers between devices with their start and end apart: 12, of which 1 were waited for; matrix products, arithmetic and copies ran while one was open for 0% of the time, Pallas kernels for 0%

profile of v1, /device:TPU:33, one launch (start us, length us, event | category | flops | bytes accessed | tf_op | source)
XLA Modules:
  0.0 136.7 jit_solution(4542291584928539785)
XLA Ops:
  0.6 0.0 copy-start
  0.7 0.7 copy-done
  1.4 0.7 broadcast_in_dim.23
  2.1 58.8 %all-to-all-start = ((bf16[8,8,1024]{2,1,0:T(8,128)(2,1)}), bf16[8,8,1024]{2,1,0:T(8,128)(2,1)S(1)}, u32[]{:S(2)}, u32[]{:S(2)}) async-start(bf16[8,8,1024]{2,1,0:T(8,128)(2,1)} %broadcast_in_dim.23), calls=%async_computation | async-start | bytes 262144 | tf_op jit(solution)/shard_map/all_to_all | solution.py:102
  60.9 5.0 %collective-permute-start.2 = (bf16[136,1024]{1,0:T(8,128)(2,1)S(1)}, bf16[136,1024]{1,0:T(8,128)(2,1)S(1)}, u32[]{:S(2)}, u32[]{:S(2)}) collective-permute-start(bf16[136,1024]{1,0:T(8,128)(2,1)S(1)} %fusion.1.refs_0_), channel_id=1, source_target_pairs={{0,4},{2,6},{4,0},{6,2},{1,5},{3,7},{5,1},{7,3},{8,12},{10,14},{12... | collective-permute-start | bytes 835592 | tf_op jit(solution)/shard_map/ppermute | solution.py:25
  65.9 2.7 %collective-permute-start.1 = (bf16[136,1024]{1,0:T(8,128)(2,1)S(1)}, bf16[136,1024]{1,0:T(8,128)(2,1)S(1)}, u32[]{:S(2)}, u32[]{:S(2)}) collective-permute-start(bf16[136,1024]{1,0:T(8,128)(2,1)S(1)} %fusion.1.refs_0_), channel_id=1, source_target_pairs={{0,6},{2,0},{4,2},{6,4},{1,7},{3,1},{5,3},{7,5},{8,14},{10,8},{12,... | collective-permute-start | bytes 835592 | tf_op jit(solution)/shard_map/ppermute | solution.py:25
  68.6 2.7 %collective-permute-start = (bf16[136,1024]{1,0:T(8,128)(2,1)S(1)}, bf16[136,1024]{1,0:T(8,128)(2,1)S(1)}, u32[]{:S(2)}, u32[]{:S(2)}) collective-permute-start(bf16[136,1024]{1,0:T(8,128)(2,1)S(1)} %fusion.1.refs_0_), channel_id=1, source_target_pairs={{0,2},{2,4},{4,6},{6,0},{1,3},{3,5},{5,7},{7,1},{8,10},{10,12},{12... | collective-permute-start | bytes 835592 | tf_op jit(solution)/shard_map/ppermute | solution.py:25
  71.3 3.9 %collective-permute-start.3 = (bf16[136,1024]{1,0:T(8,128)(2,1)S(1)}, bf16[136,1024]{1,0:T(8,128)(2,1)S(1)}, u32[]{:S(2)}, u32[]{:S(2)}) collective-permute-start(bf16[136,1024]{1,0:T(8,128)(2,1)S(1)} %fusion.1.refs_0_), channel_id=1, source_target_pairs={{0,1},{1,0},{2,3},{3,2},{4,5},{5,4},{6,7},{7,6},{8,9},{9,8},{10,11... | collective-permute-start | bytes 835592 | tf_op jit(solution)/shard_map/ppermute | solution.py:25
  75.2 0.0 collective-permute-done.2.refs_3_
  75.2 3.6 %collective-permute-start.6 = (bf16[136,1024]{1,0:T(8,128)(2,1)S(1)}, bf16[136,1024]{1,0:T(8,128)(2,1)S(1)}, u32[]{:S(2)}, u32[]{:S(2)}) collective-permute-start(bf16[136,1024]{1,0:T(8,128)(2,1)S(1)} %collective-permute-done.2.refs_3_), channel_id=1, source_target_pairs={{0,1},{1,0},{2,3},{3,2},{4,5},{5,4},{6,7},{7,6},{8,9},{9,8},{10,11... | collective-permute-start | bytes 835592 | tf_op jit(solution)/shard_map/ppermute | solution.py:25
  78.9 0.0 collective-permute-done.1.refs_2_
  78.9 3.0 %collective-permute-start.5 = (bf16[136,1024]{1,0:T(8,128)(2,1)S(1)}, bf16[136,1024]{1,0:T(8,128)(2,1)S(1)}, u32[]{:S(2)}, u32[]{:S(2)}) collective-permute-start(bf16[136,1024]{1,0:T(8,128)(2,1)S(1)} %collective-permute-done.1.refs_2_), channel_id=1, source_target_pairs={{0,1},{1,0},{2,3},{3,2},{4,5},{5,4},{6,7},{7,6},{8,9},{9,8},{10,11... | collective-permute-start | bytes 835592 | tf_op jit(solution)/shard_map/ppermute | solution.py:25
  81.9 0.0 collective-permute-done.refs_1_
  81.9 2.0 %collective-permute-start.4 = (bf16[136,1024]{1,0:T(8,128)(2,1)S(1)}, bf16[136,1024]{1,0:T(8,128)(2,1)S(1)}, u32[]{:S(2)}, u32[]{:S(2)}) collective-permute-start(bf16[136,1024]{1,0:T(8,128)(2,1)S(1)} %collective-permute-done.refs_1_), channel_id=1, source_target_pairs={{0,1},{1,0},{2,3},{3,2},{4,5},{5,4},{6,7},{7,6},{8,9},{9,8},{10,11... | collective-permute-start | bytes 835592 | tf_op jit(solution)/shard_map/ppermute | solution.py:25
  83.9 0.0 all-to-all-done.refs_8_
  83.9 3.5 %collective-permute-start.10 = (bf16[8,8,1024]{2,1,0:T(8,128)(2,1)S(1)}, bf16[8,8,1024]{2,1,0:T(8,128)(2,1)S(1)}, u32[]{:S(2)}, u32[]{:S(2)}) collective-permute-start(bf16[8,8,1024]{2,1,0:T(8,128)(2,1)S(1)} %all-to-all-done.refs_8_), channel_id=1, source_target_pairs={{0,8},{8,16},{16,24},{24,32},{32,40},{40,48},{48,56},{56,64},{64,7... | collective-permute-start | bytes 393224 | tf_op jit(solution)/shard_map/ppermute | solution.py:25
  87.4 0.0 collective-permute-done.3.refs_4_
  87.4 3.0 %collective-permute-start.7 = (bf16[8,8,1024]{2,1,0:T(8,128)(2,1)S(1)}, bf16[8,8,1024]{2,1,0:T(8,128)(2,1)S(1)}, u32[]{:S(2)}, u32[]{:S(2)}) collective-permute-start(bf16[8,8,1024]{2,1,0:T(8,128)(2,1)S(1)} %all-to-all-done.refs_8_), channel_id=1, source_target_pairs={{0,248},{8,0},{16,8},{24,16},{32,24},{40,32},{48,40},{56,48},{64,5... | collective-permute-start | bytes 393224 | tf_op jit(solution)/shard_map/ppermute | solution.py:25
  90.5 0.0 collective-permute-done.6.refs_7_
  90.5 3.8 %collective-permute-start.9 = (bf16[4,8,1024]{2,1,0:T(8,128)(2,1)S(1)}, bf16[4,8,1024]{2,1,0:T(8,128)(2,1)S(1)}, u32[]{:S(2)}, u32[]{:S(2)}) collective-permute-start(bf16[4,8,1024]{2,1,0:T(8,128)(2,1)S(1)} %get-tuple-element.6), channel_id=1, source_target_pairs={{0,16},{8,24},{16,32},{24,40},{32,48},{40,56},{48,64},{56,72},{64,... | collective-permute-start | bytes 196616 | tf_op jit(solution)/shard_map/ppermute | solution.py:25
  94.3 0.0 collective-permute-done.5.refs_6_
  94.3 3.7 %collective-permute-start.8 = (bf16[4,8,1024]{2,1,0:T(8,128)(2,1)S(1)}, bf16[4,8,1024]{2,1,0:T(8,128)(2,1)S(1)}, u32[]{:S(2)}, u32[]{:S(2)}) collective-permute-start(bf16[4,8,1024]{2,1,0:T(8,128)(2,1)S(1)} %get-tuple-element.7), channel_id=1, source_target_pairs={{0,240},{8,248},{16,0},{24,8},{32,16},{40,24},{48,32},{56,40},{64,... | collective-permute-start | bytes 196616 | tf_op jit(solution)/shard_map/ppermute | solution.py:25
  98.0 0.0 collective-permute-done.4.refs_5_
  98.1 2.4 %collective-permute-done.8.refs_10_ = bf16[4,8,1024]{2,1,0:T(8,128)(2,1)S(1)} collective-permute-done((bf16[4,8,1024]{2,1,0:T(8,128)(2,1)S(1)}, bf16[4,8,1024]{2,1,0:T(8,128)(2,1)S(1)}, u32[]{:S(2)}, u32[]{:S(2)}) %collective-permute-start.8) | collective-permute-done | bytes 65568 | tf_op jit(solution)/shard_map/ppermute | solution.py:25
  100.4 0.0 collective-permute-done.10.refs_12_
  100.4 0.0 collective-permute-done.7.refs_9_
  100.5 0.5 copy-done.14
  101.0 0.1 copy-done.11
  101.1 0.1 copy-done.12
  101.2 4.4 %scores.1 = f32[64,128]{1,0:T(8,128)} custom-call(s32[1]{0:T(128)} %bitcast.shift_ref, f32[1,128]{1,0:T(1,128)} %bitcast.12, bf16[136,1024]{1,0:T(8,128)(2,1)} %copy-done.2, bf16[136,1024]{1,0:T(8,128)(2,1)} %copy-done.5, bf16[136,1024]{1,0:T(8,128)(2,1)} %copy-done.4, bf16[136,1024]{1,0:T(8,128)(2,1)} %copy-done.3, bf16[136,1024]{1,0:T(8,128)(2,1)} %copy-done.6, ...), custom_call_target="tpu_custom_call" | custom-call | tf_op jit(solution)/shard_map/scores/pallas_call | solution.py:113
  105.6 29.7 %all_to_all.16 = f32[64,1,128]{2,1,0:T(1,128)} all-to-all(f32[64,1,128]{2,1,0:T(1,128)} %bitcast.10), channel_id=1, replica_groups={{128,160,192,224,0,32,64,96,136,168,200,232,8,40,72,104,144,176,208,240..., dimensions={0} | all-to-all | bytes 65536 | tf_op jit(solution)/shard_map/all_to_all | solution.py:141
  135.3 1.4 %finish.1 = (f32[1,16]{1,0:T(1,128)}, f32[1,16]{1,0:T(1,128)}) custom-call(f32[64,128]{1,0:T(8,128)} %bitcast.11), custom_call_target="tpu_custom_call" | custom-call | tf_op jit(solution)/shard_map/finish/pallas_call | solution.py:142
  (34 shorter events, 0.1 us)
Async XLA Ops:
  0.6 0.8 copy-start
  0.6 60.3 %copy-start.10 = (bf16[128,1024]{1,0:T(8,128)(2,1)S(1)}, bf16[128,1024]{1,0:T(8,128)(2,1)}, u32[]{:S(2)}) copy-start(bf16[128,1024]{1,0:T(8,128)(2,1)} %param.6) | copy-start | bytes 786436
  2.1 58.8 %copy-start.15 = (s32[128]{0:T(128)S(1)}, s32[128]{0:T(128)}, u32[]{:S(2)}) copy-start(s32[128]{0:T(128)} %param.7) | copy-start | bytes 1540
  2.1 58.8 %copy-start.16 = (s32[128]{0:T(128)S(1)}, s32[128]{0:T(128)}, u32[]{:S(2)}) copy-start(s32[128]{0:T(128)} %param.8) | copy-start | bytes 1540
  2.1 81.8 %all-to-all-start = ((bf16[8,8,1024]{2,1,0:T(8,128)(2,1)}), bf16[8,8,1024]{2,1,0:T(8,128)(2,1)S(1)}, u32[]{:S(2)}, u32[]{:S(2)}) async-start(bf16[8,8,1024]{2,1,0:T(8,128)(2,1)} %broadcast_in_dim.23), calls=%async_computation | async-start | bytes 262144 | tf_op jit(solution)/shard_map/all_to_all | solution.py:102
  60.9 39.5 %copy-start.2 = (bf16[136,1024]{1,0:T(8,128)(2,1)}, bf16[136,1024]{1,0:T(8,128)(2,1)S(1)}, u32[]{:S(2)}) copy-start(bf16[136,1024]{1,0:T(8,128)(2,1)S(1)} %fusion.1.refs_0_) | copy-start | bytes 835588
  60.9 14.3 %collective-permute-start.2 = (bf16[136,1024]{1,0:T(8,128)(2,1)S(1)}, bf16[136,1024]{1,0:T(8,128)(2,1)S(1)}, u32[]{:S(2)}, u32[]{:S(2)}) collective-permute-start(bf16[136,1024]{1,0:T(8,128)(2,1)S(1)} %fusion.1.refs_0_), channel_id=1, source_target_pairs={{0,4},{2,6},{4,0},{6,2},{1,5},{3,7},{5,1},{7,3},{8,12},{10,14},{12... | collective-permute-start | bytes 835592 | tf_op jit(solution)/shard_map/ppermute | solution.py:25
  65.9 13.0 %collective-permute-start.1 = (bf16[136,1024]{1,0:T(8,128)(2,1)S(1)}, bf16[136,1024]{1,0:T(8,128)(2,1)S(1)}, u32[]{:S(2)}, u32[]{:S(2)}) collective-permute-start(bf16[136,1024]{1,0:T(8,128)(2,1)S(1)} %fusion.1.refs_0_), channel_id=1, source_target_pairs={{0,6},{2,0},{4,2},{6,4},{1,7},{3,1},{5,3},{7,5},{8,14},{10,8},{12,... | collective-permute-start | bytes 835592 | tf_op jit(solution)/shard_map/ppermute | solution.py:25
  68.6 13.3 %collective-permute-start = (bf16[136,1024]{1,0:T(8,128)(2,1)S(1)}, bf16[136,1024]{1,0:T(8,128)(2,1)S(1)}, u32[]{:S(2)}, u32[]{:S(2)}) collective-permute-start(bf16[136,1024]{1,0:T(8,128)(2,1)S(1)} %fusion.1.refs_0_), channel_id=1, source_target_pairs={{0,2},{2,4},{4,6},{6,0},{1,3},{3,5},{5,7},{7,1},{8,10},{10,12},{12... | collective-permute-start | bytes 835592 | tf_op jit(solution)/shard_map/ppermute | solution.py:25
  71.3 16.2 %collective-permute-start.3 = (bf16[136,1024]{1,0:T(8,128)(2,1)S(1)}, bf16[136,1024]{1,0:T(8,128)(2,1)S(1)}, u32[]{:S(2)}, u32[]{:S(2)}) collective-permute-start(bf16[136,1024]{1,0:T(8,128)(2,1)S(1)} %fusion.1.refs_0_), channel_id=1, source_target_pairs={{0,1},{1,0},{2,3},{3,2},{4,5},{5,4},{6,7},{7,6},{8,9},{9,8},{10,11... | collective-permute-start | bytes 835592 | tf_op jit(solution)/shard_map/ppermute | solution.py:25
  75.2 25.2 %copy-start.3 = (bf16[136,1024]{1,0:T(8,128)(2,1)}, bf16[136,1024]{1,0:T(8,128)(2,1)S(1)}, u32[]{:S(2)}) copy-start(bf16[136,1024]{1,0:T(8,128)(2,1)S(1)} %collective-permute-done.2.refs_3_) | copy-start | bytes 835588
  75.2 15.3 %collective-permute-start.6 = (bf16[136,1024]{1,0:T(8,128)(2,1)S(1)}, bf16[136,1024]{1,0:T(8,128)(2,1)S(1)}, u32[]{:S(2)}, u32[]{:S(2)}) collective-permute-start(bf16[136,1024]{1,0:T(8,128)(2,1)S(1)} %collective-permute-done.2.refs_3_), channel_id=1, source_target_pairs={{0,1},{1,0},{2,3},{3,2},{4,5},{5,4},{6,7},{7,6},{8,9},{9,8},{10,11... | collective-permute-start | bytes 835592 | tf_op jit(solution)/shard_map/ppermute | solution.py:25
  78.9 21.6 %copy-start.4 = (bf16[136,1024]{1,0:T(8,128)(2,1)}, bf16[136,1024]{1,0:T(8,128)(2,1)S(1)}, u32[]{:S(2)}) copy-start(bf16[136,1024]{1,0:T(8,128)(2,1)S(1)} %collective-permute-done.1.refs_2_) | copy-start | bytes 835588
  78.9 15.4 %collective-permute-start.5 = (bf16[136,1024]{1,0:T(8,128)(2,1)S(1)}, bf16[136,1024]{1,0:T(8,128)(2,1)S(1)}, u32[]{:S(2)}, u32[]{:S(2)}) collective-permute-start(bf16[136,1024]{1,0:T(8,128)(2,1)S(1)} %collective-permute-done.1.refs_2_), channel_id=1, source_target_pairs={{0,1},{1,0},{2,3},{3,2},{4,5},{5,4},{6,7},{7,6},{8,9},{9,8},{10,11... | collective-permute-start | bytes 835592 | tf_op jit(solution)/shard_map/ppermute | solution.py:25
  81.9 18.6 %copy-start.5 = (bf16[136,1024]{1,0:T(8,128)(2,1)}, bf16[136,1024]{1,0:T(8,128)(2,1)S(1)}, u32[]{:S(2)}) copy-start(bf16[136,1024]{1,0:T(8,128)(2,1)S(1)} %collective-permute-done.refs_1_) | copy-start | bytes 835588
  81.9 16.1 %collective-permute-start.4 = (bf16[136,1024]{1,0:T(8,128)(2,1)S(1)}, bf16[136,1024]{1,0:T(8,128)(2,1)S(1)}, u32[]{:S(2)}, u32[]{:S(2)}) collective-permute-start(bf16[136,1024]{1,0:T(8,128)(2,1)S(1)} %collective-permute-done.refs_1_), channel_id=1, source_target_pairs={{0,1},{1,0},{2,3},{3,2},{4,5},{5,4},{6,7},{7,6},{8,9},{9,8},{10,11... | collective-permute-start | bytes 835592 | tf_op jit(solution)/shard_map/ppermute | solution.py:25
  83.9 6.6 %copy-start.1 = (bf16[8,8,1024]{2,1,0:T(8,128)(2,1)}, bf16[8,8,1024]{2,1,0:T(8,128)(2,1)S(1)}, u32[]{:S(2)}) copy-start(bf16[8,8,1024]{2,1,0:T(8,128)(2,1)S(1)} %all-to-all-done.refs_8_) | copy-start | bytes 393220
  83.9 16.5 %collective-permute-start.10 = (bf16[8,8,1024]{2,1,0:T(8,128)(2,1)S(1)}, bf16[8,8,1024]{2,1,0:T(8,128)(2,1)S(1)}, u32[]{:S(2)}, u32[]{:S(2)}) collective-permute-start(bf16[8,8,1024]{2,1,0:T(8,128)(2,1)S(1)} %all-to-all-done.refs_8_), channel_id=1, source_target_pairs={{0,8},{8,16},{16,24},{24,32},{32,40},{40,48},{48,56},{56,64},{64,7... | collective-permute-start | bytes 393224 | tf_op jit(solution)/shard_map/ppermute | solution.py:25
  87.4 13.0 %copy-start.6 = (bf16[136,1024]{1,0:T(8,128)(2,1)}, bf16[136,1024]{1,0:T(8,128)(2,1)S(1)}, u32[]{:S(2)}) copy-start(bf16[136,1024]{1,0:T(8,128)(2,1)S(1)} %collective-permute-done.3.refs_4_) | copy-start | bytes 835588
  87.4 13.0 %collective-permute-start.7 = (bf16[8,8,1024]{2,1,0:T(8,128)(2,1)S(1)}, bf16[8,8,1024]{2,1,0:T(8,128)(2,1)S(1)}, u32[]{:S(2)}, u32[]{:S(2)}) collective-permute-start(bf16[8,8,1024]{2,1,0:T(8,128)(2,1)S(1)} %all-to-all-done.refs_8_), channel_id=1, source_target_pairs={{0,248},{8,0},{16,8},{24,16},{32,24},{40,32},{48,40},{56,48},{64,5... | collective-permute-start | bytes 393224 | tf_op jit(solution)/shard_map/ppermute | solution.py:25
  90.5 10.0 %copy-start.7 = (bf16[136,1024]{1,0:T(8,128)(2,1)}, bf16[136,1024]{1,0:T(8,128)(2,1)S(1)}, u32[]{:S(2)}) copy-start(bf16[136,1024]{1,0:T(8,128)(2,1)S(1)} %collective-permute-done.6.refs_7_) | copy-start | bytes 835588
  90.5 7.5 %collective-permute-start.9 = (bf16[4,8,1024]{2,1,0:T(8,128)(2,1)S(1)}, bf16[4,8,1024]{2,1,0:T(8,128)(2,1)S(1)}, u32[]{:S(2)}, u32[]{:S(2)}) collective-permute-start(bf16[4,8,1024]{2,1,0:T(8,128)(2,1)S(1)} %get-tuple-element.6), channel_id=1, source_target_pairs={{0,16},{8,24},{16,32},{24,40},{32,48},{40,56},{48,64},{56,72},{64,... | collective-permute-start | bytes 196616 | tf_op jit(solution)/shard_map/ppermute | solution.py:25
  94.3 6.2 %copy-start.8 = (bf16[136,1024]{1,0:T(8,128)(2,1)}, bf16[136,1024]{1,0:T(8,128)(2,1)S(1)}, u32[]{:S(2)}) copy-start(bf16[136,1024]{1,0:T(8,128)(2,1)S(1)} %collective-permute-done.5.refs_6_) | copy-start | bytes 835588
  94.3 6.1 %collective-permute-start.8 = (bf16[4,8,1024]{2,1,0:T(8,128)(2,1)S(1)}, bf16[4,8,1024]{2,1,0:T(8,128)(2,1)S(1)}, u32[]{:S(2)}, u32[]{:S(2)}) collective-permute-start(bf16[4,8,1024]{2,1,0:T(8,128)(2,1)S(1)} %get-tuple-element.7), channel_id=1, source_target_pairs={{0,240},{8,248},{16,0},{24,8},{32,16},{40,24},{48,32},{56,40},{64,... | collective-permute-start | bytes 196616 | tf_op jit(solution)/shard_map/ppermute | solution.py:25
  98.0 2.5 %copy-start.9 = (bf16[136,1024]{1,0:T(8,128)(2,1)}, bf16[136,1024]{1,0:T(8,128)(2,1)S(1)}, u32[]{:S(2)}) copy-start(bf16[136,1024]{1,0:T(8,128)(2,1)S(1)} %collective-permute-done.4.refs_5_) | copy-start | bytes 835588
  98.1 2.5 %copy-start.13 = (bf16[4,8,1024]{2,1,0:T(8,128)(2,1)}, bf16[4,8,1024]{2,1,0:T(8,128)(2,1)S(1)}, u32[]{:S(2)}) copy-start(bf16[4,8,1024]{2,1,0:T(8,128)(2,1)S(1)} %collective-permute-done.9.refs_11_) | copy-start | bytes 196612
  100.4 0.6 copy-start.14
  100.4 0.7 copy-start.11
  100.4 0.7 copy-start.12

commit v2 on v1

--- a/solution.py
+++ b/solution.py
@@ -10,14 +10,15 @@
 ROW = 4
 RESIDUES = 4
 LOOP = RING // RESIDUES
-FIRST = RING // 2
+FIRST = RING - RESIDUES
+LAST = RING // 2
 LOW = -1e30
 
 GROUP = ("ring", "row", "merge")
 
 
-def ring_place(residue, step):
-    return (FIRST + RESIDUES * step + residue) % RING
+def ring_place(residue, step, start=FIRST):
+    return (start + RESIDUES * step + residue) % RING
 
 
 def shifted(value, axis, by):
@@ -25,9 +26,19 @@
     return lax.ppermute(value, axis, [(k, (k + by) % size) for k in range(size)])
 
 
+def mirrored(value, mask):
+    size = lax.axis_size("row")
+    return lax.ppermute(value, "row", [(k, k ^ mask) for k in range(size)])
+
+
+def in_vmem(value):
+    return pltpu.with_memory_space_constraint(value, pltpu.MemorySpace.VMEM)
+
+
 def scores_kernel(shift_ref, bias_ref, *refs):
-    packs, pieces, out_ref = refs[:8], refs[8:13], refs[13]
-    rows_ref, sims_ref = refs[14:]
+    pairs, pieces, out_ref = refs[:4], refs[4:9], refs[9]
+    rows_ref, sims_ref = refs[10:]
+    packs = [pair.at[k] for pair in pairs for k in range(2)]
     rows = out_ref.shape[0] // 2
     at = 0
     for piece in pieces:
@@ -54,7 +65,8 @@
     lane = lax.broadcasted_iota(jnp.int32, (rows, at), 1)
     line = lax.broadcasted_iota(jnp.int32, (rows, at), 0)
     per = 8 * LOOP
-    slot = ((lane // per + shift_ref[0]) % RESIDUES) * LOOP + (lane // 8) % LOOP
+    turn = (LAST - FIRST) // RESIDUES
+    slot = ((lane // per + shift_ref[0]) % RESIDUES) * LOOP + (lane // 8 + LOOP - turn) % LOOP
     mine = slot == line
     query = lax.broadcasted_iota(jnp.int32, (at, 128), 0) % 8
     column = lax.broadcasted_iota(jnp.int32, (at, 128), 1)
@@ -102,8 +114,9 @@
     near = lax.all_to_all(
         jnp.broadcast_to(mine[None], (LOOP, *mine.shape)), "ring", 0, 0, axis_index_groups=loops, tiled=True
     )
-    row_packs = [pack, shifted(pack, "row", 1), shifted(pack, "row", -1), shifted(pack, "row", 2)]
-    packs = row_packs + [shifted(one, "merge", 1) for one in row_packs]
+    two = jnp.stack([pack, mirrored(pack, 1)])
+    four = [two, mirrored(two, 3)]
+    pairs = four + [shifted(one, "merge", 1) for one in four]
     up = shifted(near, "ring", -1)
     down = shifted(near, "ring", 1)
     far_up = shifted(near[: LOOP // 2], "ring", -2)
@@ -113,7 +126,7 @@
     stats = pl.pallas_call(
         scores_kernel,
         out_shape=jax.ShapeDtypeStruct((slots, 128), jnp.float32),
-        in_specs=[pl.BlockSpec(memory_space=pltpu.SMEM)] + [pl.BlockSpec(memory_space=pltpu.VMEM)] * 14,
+        in_specs=[pl.BlockSpec(memory_space=pltpu.SMEM)] + [pl.BlockSpec(memory_space=pltpu.VMEM)] * 10,
         out_specs=pl.BlockSpec(memory_space=pltpu.VMEM),
         scratch_shapes=[
             pltpu.VMEM((RING * half, spans.shape[1]), jnp.bfloat16),
@@ -123,15 +136,11 @@
     )(
         (place % RESIDUES).astype(jnp.int32)[None],
         doc_bias[None, :],
-        *packs,
-        near,
-        up,
-        far_up,
-        far_down,
-        down,
+        *[in_vmem(pair) for pair in pairs],
+        *[in_vmem(piece) for piece in (near, up, far_up, far_down, down)],
     )
     owners = [
-        (ring_place(r, i) * ROW + x) * 2 + m
+        (ring_place(r, i, LAST) * ROW + x) * 2 + m
         for x in range(ROW)
         for m in range(2)
         for r in range(RESIDUES)
@@ -145,7 +154,7 @@
         in_specs=[pl.BlockSpec(memory_space=pltpu.VMEM)],
         out_specs=[pl.BlockSpec(memory_space=pltpu.VMEM)] * 2,
         name="finish",
-    )(got)
+    )(in_vmem(got))
     return soft.reshape(-1), top.reshape(-1)
 
 

time: 137 us -> 128 us (0.934)
  starting transfers between devices: 95.6 us -> 79.7 us
  waiting for transfers between devices: 2.38 us -> 10.3 us
  Pallas kernels: 5.87 us -> 4.06 us
  other arithmetic: 0.03 us -> 1.74 us
  local copies, waits for them, and re-layouts: 2.1 us -> 0.69 us
    all_to_all x1, starting transfers between devices: 58.8 us -> 45.2 us  [shards(): lax.all_to_all(jnp.broadcast_to(mine[None], (LOOP, *mine.shape)), 'ring',...]
    ppermute x11 -> x6, starting transfers between devices: 36.8 us -> 26.5 us  [shifted(): lax.ppermute(value, axis, [(k, (k + by) % size) for k in range(size)])]
    ppermute x0 -> x2, waiting for transfers between devices: none -> 8.69 us  [mirrored(): return lax.ppermute(value, 'row', [(k, k ^ mask) for k in range(size)])]
    ppermute x0 -> x2, starting transfers between devices: none -> 7.99 us  [mirrored(): return lax.ppermute(value, 'row', [(k, k ^ mask) for k in range(size)])]
    unnamed x34 -> x2, local copies, waits for them, and re-layouts: 1.43 us -> 0.01 us
  transfers between devices with their start and end apart: 12 -> 9, of which waited for: 1 -> 2; matrix products, arithmetic and copies ran while one was open for 0% -> 1% of each run, Pallas kernels for 0% -> 0%
where the time goes in v2:
time: 128 us; the launch traced here: 127 us
  starting transfers between devices  79.7 us (62%)
  blocking collectives  30.1 us (24%)
  waiting for transfers between devices  10.3 us (8%)
  Pallas kernels  4.06 us (3%)
  other arithmetic  1.74 us (1%)
    all_to_all x1, starting transfers between devices, shards(): lax.all_to_all(jnp.broadcast_to(mine[None], (LOOP, *mine.shape)), 'ring',...  45.2 us
    all_to_all x1, blocking collectives, shards(): lax.all_to_all(stats, GROUP, 0, 0, axis_index_groups=columns, tiled=True)  30.1 us
    ppermute x6, starting transfers between devices, shifted(): lax.ppermute(value, axis, [(k, (k + by) % size) for k in range(size)])  26.5 us
    ppermute x2, waiting for transfers between devices, mirrored(): return lax.ppermute(value, 'row', [(k, k ^ mask) for k in range(size)])  8.69 us
    ppermute x2, starting transfers between devices, mirrored(): return lax.ppermute(value, 'row', [(k, k ^ mask) for k in range(size)])  7.99 us
    pallas_call x1, Pallas kernels, shards(): pl.pallas_call(scores_kernel, out_shape=jax.ShapeDtypeStruct((slots, 128)...  3.39 us
  transfers between devices with their start and end apart: 9, of which 2 were waited for; matrix products, arithmetic and copies ran while one was open for 1% of the time, Pallas kernels for 0%

profile of v2, /device:TPU:33, one launch (start us, length us, event | category | flops | bytes accessed | tf_op | source)
XLA Modules:
  0.0 127.3 jit_solution(8548455285535659583)
XLA Ops:
  0.6 0.0 copy-start
  0.6 0.7 fusion.3
  1.3 1.0 fusion.4
  2.3 4.1 %collective-permute-start = (bf16[136,1024]{1,0:T(8,128)(2,1)S(1)}, bf16[136,1024]{1,0:T(8,128)(2,1)S(1)}, u32[]{:S(2)}, u32[]{:S(2)}) collective-permute-start(bf16[136,1024]{1,0:T(8,128)(2,1)S(1)} %get-tuple-element.7), channel_id=1, source_target_pairs={{0,2},{2,0},{4,6},{6,4},{1,3},{3,1},{5,7},{7,5},{8,10},{10,8},{12,... | collective-permute-start | bytes 835592 | tf_op jit(solution)/shard_map/ppermute | solution.py:31
  6.5 0.0 copy-done
  6.5 0.7 broadcast_in_dim.23
  7.1 45.2 %all-to-all-start = ((bf16[8,8,1024]{2,1,0:T(8,128)(2,1)}), bf16[8,8,1024]{2,1,0:T(8,128)(2,1)S(1)}, u32[]{:S(2)}, u32[]{:S(2)}) async-start(bf16[8,8,1024]{2,1,0:T(8,128)(2,1)} %broadcast_in_dim.23), calls=%async_computation | async-start | bytes 262144 | tf_op jit(solution)/shard_map/all_to_all | solution.py:114
  52.3 0.0 collective-permute-done
  52.3 0.1 pad_maximum_fusion.refs_0_
  52.4 3.9 %collective-permute-start.1 = (bf16[2,136,1024]{2,1,0:T(8,128)(2,1)S(1)}, bf16[2,136,1024]{2,1,0:T(8,128)(2,1)S(1)}, u32[]{:S(2)}, u32[]{:S(2)}) collective-permute-start(bf16[2,136,1024]{2,1,0:T(8,128)(2,1)S(1)} %pad_maximum_fusion.refs_0_), channel_id=1, source_target_pairs={{0,6},{2,4},{4,2},{6,0},{1,7},{3,5},{5,3},{7,1},{8,14},{10,12},{12... | collective-permute-start | bytes 1671176 | tf_op jit(solution)/shard_map/ppermute | solution.py:31
  56.3 3.4 %collective-permute-start.2 = (bf16[2,136,1024]{2,1,0:T(8,128)(2,1)S(1)}, bf16[2,136,1024]{2,1,0:T(8,128)(2,1)S(1)}, u32[]{:S(2)}, u32[]{:S(2)}) collective-permute-start(bf16[2,136,1024]{2,1,0:T(8,128)(2,1)S(1)} %pad_maximum_fusion.refs_0_), channel_id=1, source_target_pairs={{0,1},{1,0},{2,3},{3,2},{4,5},{5,4},{6,7},{7,6},{8,9},{9,8},{10,11... | collective-permute-start | bytes 1671176 | tf_op jit(solution)/shard_map/ppermute | solution.py:26
  59.7 8.7 %collective-permute-done.1.refs_1_ = bf16[2,136,1024]{2,1,0:T(8,128)(2,1)S(1)} collective-permute-done((bf16[2,136,1024]{2,1,0:T(8,128)(2,1)S(1)}, bf16[2,136,1024]{2,1,0:T(8,128)(2,1)S(1)}, u32[]{:S(2)}, u32[]{:S(2)}) %collective-permute-start.1) | collective-permute-done | bytes 557088 | tf_op jit(solution)/shard_map/ppermute | solution.py:31
  68.3 4.1 %collective-permute-start.3 = (bf16[2,136,1024]{2,1,0:T(8,128)(2,1)S(1)}, bf16[2,136,1024]{2,1,0:T(8,128)(2,1)S(1)}, u32[]{:S(2)}, u32[]{:S(2)}) collective-permute-start(bf16[2,136,1024]{2,1,0:T(8,128)(2,1)S(1)} %collective-permute-done.1.refs_1_), channel_id=1, source_target_pairs={{0,1},{1,0},{2,3},{3,2},{4,5},{5,4},{6,7},{7,6},{8,9},{9,8},{10,11... | collective-permute-start | bytes 1671176 | tf_op jit(solution)/shard_map/ppermute | solution.py:26
  72.5 0.0 all-to-all-done.refs_4_
  72.5 4.6 %collective-permute-start.7 = (bf16[8,8,1024]{2,1,0:T(8,128)(2,1)S(1)}, bf16[8,8,1024]{2,1,0:T(8,128)(2,1)S(1)}, u32[]{:S(2)}, u32[]{:S(2)}) collective-permute-start(bf16[8,8,1024]{2,1,0:T(8,128)(2,1)S(1)} %all-to-all-done.refs_4_), channel_id=1, source_target_pairs={{0,8},{8,16},{16,24},{24,32},{32,40},{40,48},{48,56},{56,64},{64,7... | collective-permute-start | bytes 393224 | tf_op jit(solution)/shard_map/ppermute | solution.py:26
  77.1 3.4 %collective-permute-start.4 = (bf16[8,8,1024]{2,1,0:T(8,128)(2,1)S(1)}, bf16[8,8,1024]{2,1,0:T(8,128)(2,1)S(1)}, u32[]{:S(2)}, u32[]{:S(2)}) collective-permute-start(bf16[8,8,1024]{2,1,0:T(8,128)(2,1)S(1)} %all-to-all-done.refs_4_), channel_id=1, source_target_pairs={{0,248},{8,0},{16,8},{24,16},{32,24},{40,32},{48,40},{56,48},{64,5... | collective-permute-start | bytes 393224 | tf_op jit(solution)/shard_map/ppermute | solution.py:26
  80.5 2.9 %collective-permute-start.6 = (bf16[4,8,1024]{2,1,0:T(8,128)(2,1)S(1)}, bf16[4,8,1024]{2,1,0:T(8,128)(2,1)S(1)}, u32[]{:S(2)}, u32[]{:S(2)}) collective-permute-start(bf16[4,8,1024]{2,1,0:T(8,128)(2,1)S(1)} %get-tuple-element.8), channel_id=1, source_target_pairs={{0,16},{8,24},{16,32},{24,40},{32,48},{40,56},{48,64},{56,72},{64,... | collective-permute-start | bytes 196616 | tf_op jit(solution)/shard_map/ppermute | solution.py:26
  83.5 0.0 collective-permute-done.2.refs_2_
  83.5 8.1 %collective-permute-start.5 = (bf16[4,8,1024]{2,1,0:T(8,128)(2,1)S(1)}, bf16[4,8,1024]{2,1,0:T(8,128)(2,1)S(1)}, u32[]{:S(2)}, u32[]{:S(2)}) collective-permute-start(bf16[4,8,1024]{2,1,0:T(8,128)(2,1)S(1)} %get-tuple-element.9), channel_id=1, source_target_pairs={{0,240},{8,248},{16,0},{24,8},{32,16},{40,24},{48,32},{56,40},{64,... | collective-permute-start | bytes 196616 | tf_op jit(solution)/shard_map/ppermute | solution.py:26
  91.5 0.0 collective-permute-done.6.refs_7_
  91.6 1.6 %collective-permute-done.5.refs_6_ = bf16[4,8,1024]{2,1,0:T(8,128)(2,1)S(1)} collective-permute-done((bf16[4,8,1024]{2,1,0:T(8,128)(2,1)S(1)}, bf16[4,8,1024]{2,1,0:T(8,128)(2,1)S(1)}, u32[]{:S(2)}, u32[]{:S(2)}) %collective-permute-start.5) | collective-permute-done | bytes 65568 | tf_op jit(solution)/shard_map/ppermute | solution.py:26
  93.2 0.0 collective-permute-done.7.refs_8_
  93.2 0.0 collective-permute-done.4.refs_5_
  93.2 0.0 collective-permute-done.3.refs_3_
  93.2 3.4 %scores.1 = f32[64,128]{1,0:T(8,128)} custom-call(s32[1]{0:T(128)} %bitcast.shift_ref, f32[1,128]{1,0:T(1,128)} %bitcast.16, bf16[2,136,1024]{2,1,0:T(8,128)(2,1)S(1)} %pad_maximum_fusion.refs_0_, bf16[2,136,1024]{2,1,0:T(8,128)(2,1)S(1)} %collective-permute-done.1.refs_1_, bf16[2,136,1024]{2,1,0:T(8,128)(2,1)S(1)} %collective-permute-done.2.refs_2_, ...), custom_call_target="tpu_custom_call" | custom-call | tf_op jit(solution)/shard_map/scores/pallas_call | solution.py:126
  96.6 30.1 %all_to_all.16 = f32[64,1,128]{2,1,0:T(1,128)S(1)} all-to-all(f32[64,1,128]{2,1,0:T(1,128)} %bitcast.15), channel_id=1, replica_groups={{128,160,192,224,0,32,64,96,136,168,200,232,8,40,72,104,144,176,208,240..., dimensions={0} | all-to-all | bytes 65536 | tf_op jit(solution)/shard_map/all_to_all | solution.py:150
  126.6 0.7 finish.1
  (2 shorter events, 0.0 us)
Async XLA Ops:
  0.6 5.8 %copy-start = (bf16[16,1024]{1,0:T(8,128)(2,1)S(1)}, bf16[16,1024]{1,0:T(8,128)(2,1)}, u32[]{:S(2)}) copy-start(bf16[16,1024]{1,0:T(8,128)(2,1)} %param.5) | copy-start | bytes 98308
  2.3 50.0 %collective-permute-start = (bf16[136,1024]{1,0:T(8,128)(2,1)S(1)}, bf16[136,1024]{1,0:T(8,128)(2,1)S(1)}, u32[]{:S(2)}, u32[]{:S(2)}) collective-permute-start(bf16[136,1024]{1,0:T(8,128)(2,1)S(1)} %get-tuple-element.7), channel_id=1, source_target_pairs={{0,2},{2,0},{4,6},{6,4},{1,3},{3,1},{5,7},{7,5},{8,10},{10,8},{12,... | collective-permute-start | bytes 835592 | tf_op jit(solution)/shard_map/ppermute | solution.py:31
  7.1 65.3 %all-to-all-start = ((bf16[8,8,1024]{2,1,0:T(8,128)(2,1)}), bf16[8,8,1024]{2,1,0:T(8,128)(2,1)S(1)}, u32[]{:S(2)}, u32[]{:S(2)}) async-start(bf16[8,8,1024]{2,1,0:T(8,128)(2,1)} %broadcast_in_dim.23), calls=%async_computation | async-start | bytes 262144 | tf_op jit(solution)/shard_map/all_to_all | solution.py:114
  52.4 16.0 %collective-permute-start.1 = (bf16[2,136,1024]{2,1,0:T(8,128)(2,1)S(1)}, bf16[2,136,1024]{2,1,0:T(8,128)(2,1)S(1)}, u32[]{:S(2)}, u32[]{:S(2)}) collective-permute-start(bf16[2,136,1024]{2,1,0:T(8,128)(2,1)S(1)} %pad_maximum_fusion.refs_0_), channel_id=1, source_target_pairs={{0,6},{2,4},{4,2},{6,0},{1,7},{3,5},{5,3},{7,1},{8,14},{10,12},{12... | collective-permute-start | bytes 1671176 | tf_op jit(solution)/shard_map/ppermute | solution.py:31
  56.3 27.2 %collective-permute-start.2 = (bf16[2,136,1024]{2,1,0:T(8,128)(2,1)S(1)}, bf16[2,136,1024]{2,1,0:T(8,128)(2,1)S(1)}, u32[]{:S(2)}, u32[]{:S(2)}) collective-permute-start(bf16[2,136,1024]{2,1,0:T(8,128)(2,1)S(1)} %pad_maximum_fusion.refs_0_), channel_id=1, source_target_pairs={{0,1},{1,0},{2,3},{3,2},{4,5},{5,4},{6,7},{7,6},{8,9},{9,8},{10,11... | collective-permute-start | bytes 1671176 | tf_op jit(solution)/shard_map/ppermute | solution.py:26
  68.3 24.8 %collective-permute-start.3 = (bf16[2,136,1024]{2,1,0:T(8,128)(2,1)S(1)}, bf16[2,136,1024]{2,1,0:T(8,128)(2,1)S(1)}, u32[]{:S(2)}, u32[]{:S(2)}) collective-permute-start(bf16[2,136,1024]{2,1,0:T(8,128)(2,1)S(1)} %collective-permute-done.1.refs_1_), channel_id=1, source_target_pairs={{0,1},{1,0},{2,3},{3,2},{4,5},{5,4},{6,7},{7,6},{8,9},{9,8},{10,11... | collective-permute-start | bytes 1671176 | tf_op jit(solution)/shard_map/ppermute | solution.py:26
  72.5 20.7 %collective-permute-start.7 = (bf16[8,8,1024]{2,1,0:T(8,128)(2,1)S(1)}, bf16[8,8,1024]{2,1,0:T(8,128)(2,1)S(1)}, u32[]{:S(2)}, u32[]{:S(2)}) collective-permute-start(bf16[8,8,1024]{2,1,0:T(8,128)(2,1)S(1)} %all-to-all-done.refs_4_), channel_id=1, source_target_pairs={{0,8},{8,16},{16,24},{24,32},{32,40},{40,48},{48,56},{56,64},{64,7... | collective-permute-start | bytes 393224 | tf_op jit(solution)/shard_map/ppermute | solution.py:26
  77.1 16.1 %collective-permute-start.4 = (bf16[8,8,1024]{2,1,0:T(8,128)(2,1)S(1)}, bf16[8,8,1024]{2,1,0:T(8,128)(2,1)S(1)}, u32[]{:S(2)}, u32[]{:S(2)}) collective-permute-start(bf16[8,8,1024]{2,1,0:T(8,128)(2,1)S(1)} %all-to-all-done.refs_4_), channel_id=1, source_target_pairs={{0,248},{8,0},{16,8},{24,16},{32,24},{40,32},{48,40},{56,48},{64,5... | collective-permute-start | bytes 393224 | tf_op jit(solution)/shard_map/ppermute | solution.py:26
  80.5 11.0 %collective-permute-start.6 = (bf16[4,8,1024]{2,1,0:T(8,128)(2,1)S(1)}, bf16[4,8,1024]{2,1,0:T(8,128)(2,1)S(1)}, u32[]{:S(2)}, u32[]{:S(2)}) collective-permute-start(bf16[4,8,1024]{2,1,0:T(8,128)(2,1)S(1)} %get-tuple-element.8), channel_id=1, source_target_pairs={{0,16},{8,24},{16,32},{24,40},{32,48},{40,56},{48,64},{56,72},{64,... | collective-permute-start | bytes 196616 | tf_op jit(solution)/shard_map/ppermute | solution.py:26
  83.5 9.7 %collective-permute-start.5 = (bf16[4,8,1024]{2,1,0:T(8,128)(2,1)S(1)}, bf16[4,8,1024]{2,1,0:T(8,128)(2,1)S(1)}, u32[]{:S(2)}, u32[]{:S(2)}) collective-permute-start(bf16[4,8,1024]{2,1,0:T(8,128)(2,1)S(1)} %get-tuple-element.9), channel_id=1, source_target_pairs={{0,240},{8,248},{16,0},{24,8},{32,16},{40,24},{48,32},{56,40},{64,... | collective-permute-start | bytes 196616 | tf_op jit(solution)/shard_map/ppermute | solution.py:26

commit v3 on v2

--- a/solution.py
+++ b/solution.py
@@ -5,6 +5,7 @@
 from jax.experimental.pallas import tpu as pltpu
 from jax.sharding import Mesh
 from jax.sharding import PartitionSpec as P
+
 
 RING = 32
 ROW = 4
@@ -36,8 +37,8 @@
 
 
 def scores_kernel(shift_ref, bias_ref, *refs):
-    pairs, pieces, out_ref = refs[:4], refs[4:9], refs[9]
-    rows_ref, sims_ref = refs[10:]
+    pairs, pieces, out_ref = refs[:4], refs[4:8], refs[8]
+    rows_ref, sims_ref = refs[9:]
     packs = [pair.at[k] for pair in pairs for k in range(2)]
     rows = out_ref.shape[0] // 2
     at = 0
@@ -111,22 +112,21 @@
     pack = jnp.concatenate([spans, codes], axis=0)
 
     loops = [[ring_place(r, i) for i in range(LOOP)] for r in range(RESIDUES)]
-    near = lax.all_to_all(
-        jnp.broadcast_to(mine[None], (LOOP, *mine.shape)), "ring", 0, 0, axis_index_groups=loops, tiled=True
-    )
-    two = jnp.stack([pack, mirrored(pack, 1)])
+    copies = jnp.broadcast_to(mine[None], (LOOP, *mine.shape))
+    near = lax.all_to_all(copies, "ring", 0, 0, axis_index_groups=loops, tiled=True)
+    other = mirrored(pack, 1)
+    two = jnp.stack([pack, other])
     four = [two, mirrored(two, 3)]
     pairs = four + [shifted(one, "merge", 1) for one in four]
     up = shifted(near, "ring", -1)
     down = shifted(near, "ring", 1)
-    far_up = shifted(near[: LOOP // 2], "ring", -2)
-    far_down = shifted(near[LOOP // 2 :], "ring", 2)
+    across = lax.ppermute(near, "ring", [(k, (k + 4 * (k % 2) - 2) % RING) for k in range(RING)])
 
     slots = RING * 2
     stats = pl.pallas_call(
         scores_kernel,
         out_shape=jax.ShapeDtypeStruct((slots, 128), jnp.float32),
-        in_specs=[pl.BlockSpec(memory_space=pltpu.SMEM)] + [pl.BlockSpec(memory_space=pltpu.VMEM)] * 10,
+        in_specs=[pl.BlockSpec(memory_space=pltpu.SMEM)] + [pl.BlockSpec(memory_space=pltpu.VMEM)] * 9,
         out_specs=pl.BlockSpec(memory_space=pltpu.VMEM),
         scratch_shapes=[
             pltpu.VMEM((RING * half, spans.shape[1]), jnp.bfloat16),
@@ -137,7 +137,7 @@
         (place % RESIDUES).astype(jnp.int32)[None],
         doc_bias[None, :],
         *[in_vmem(pair) for pair in pairs],
-        *[in_vmem(piece) for piece in (near, up, far_up, far_down, down)],
+        *[in_vmem(piece) for piece in (near, up, across, down)],
     )
     owners = [
         (ring_place(r, i, LAST) * ROW + x) * 2 + m

time: 128 us -> 136 us (1.062)
  waiting for transfers between devices: 10.3 us -> 18.8 us
    ppermute x6 -> x4, starting transfers between devices: 26.5 us -> 12.1 us  [shifted(): lax.ppermute(value, axis, [(k, (k + by) % size) for k in range(size)])]
    ppermute x0 -> x1, starting transfers between devices: none -> 12 us  [shards(): lax.ppermute(near, 'ring', [(k, (k + 4 * (k % 2) - 2) % RING) for k in ra...]
    all_to_all x1, waiting for transfers between devices: 0.01 us -> 11.2 us  [shards(): lax.all_to_all(copies, 'ring', 0, 0, axis_index_groups=loops, tiled=True)]
    ppermute x2, waiting for transfers between devices: 8.69 us -> 3.92 us  [mirrored(): return lax.ppermute(value, 'row', [(k, k ^ mask) for k in range(size)])]
    ppermute x2, starting transfers between devices: 7.99 us -> 11.2 us  [mirrored(): return lax.ppermute(value, 'row', [(k, k ^ mask) for k in range(size)])]
    ppermute x6 -> x4, waiting for transfers between devices: 1.61 us -> 3.75 us  [shifted(): lax.ppermute(value, axis, [(k, (k + by) % size) for k in range(size)])]
  transfers between devices with their start and end apart: 9 -> 8, of which waited for: 2 -> 3; matrix products, arithmetic and copies ran while one was open for 1% -> 0% of each run, Pallas kernels for 0% -> 0%
where the time goes in v3:
time: 136 us
  starting transfers between devices  80.6 us (59%)
  blocking collectives  29 us (21%)
  waiting for transfers between devices  18.8 us (14%)
  Pallas kernels  4.05 us (3%)
  other arithmetic  1.74 us (1%)
    all_to_all x1, starting transfers between devices, shards(): lax.all_to_all(copies, 'ring', 0, 0, axis_index_groups=loops, tiled=True)  45.2 us
    all_to_all x1, blocking collectives, shards(): lax.all_to_all(stats, GROUP, 0, 0, axis_index_groups=columns, tiled=True)  29 us
    ppermute x4, starting transfers between devices, shifted(): lax.ppermute(value, axis, [(k, (k + by) % size) for k in range(size)])  12.1 us
    ppermute x1, starting transfers between devices, shards(): lax.ppermute(near, 'ring', [(k, (k + 4 * (k % 2) - 2) % RING) for k in ra...  12 us
    ppermute x2, starting transfers between devices, mirrored(): return lax.ppermute(value, 'row', [(k, k ^ mask) for k in range(size)])  11.2 us
    all_to_all x1, waiting for transfers between devices, shards(): lax.all_to_all(copies, 'ring', 0, 0, axis_index_groups=loops, tiled=True)  11.2 us
    ppermute x2, waiting for transfers between devices, mirrored(): return lax.ppermute(value, 'row', [(k, k ^ mask) for k in range(size)])  3.92 us
    ppermute x4, waiting for transfers between devices, shifted(): lax.ppermute(value, axis, [(k, (k + by) % size) for k in range(size)])  3.75 us
  transfers between devices with their start and end apart: 8, of which 3 were waited for; matrix products, arithmetic and copies ran while one was open for 0% of the time, Pallas kernels for 0%

profile of v3, /device:TPU:33, one launch (start us, length us, event | category | flops | bytes accessed | tf_op | source)
XLA Modules:
  0.0 135.6 jit_solution(9598663571633890724)
XLA Ops:
  0.6 0.0 copy-start
  0.6 0.7 fusion.3
  1.3 1.0 fusion.4
  2.3 4.1 %collective-permute-start = (bf16[136,1024]{1,0:T(8,128)(2,1)S(1)}, bf16[136,1024]{1,0:T(8,128)(2,1)S(1)}, u32[]{:S(2)}, u32[]{:S(2)}) collective-permute-start(bf16[136,1024]{1,0:T(8,128)(2,1)S(1)} %get-tuple-element.7), channel_id=1, source_target_pairs={{0,2},{2,0},{4,6},{6,4},{1,3},{3,1},{5,7},{7,5},{8,10},{10,8},{12,... | collective-permute-start | bytes 835592 | tf_op jit(solution)/shard_map/ppermute | solution.py:32
  6.5 3.9 %collective-permute-done = bf16[136,1024]{1,0:T(8,128)(2,1)S(1)} collective-permute-done((bf16[136,1024]{1,0:T(8,128)(2,1)S(1)}, bf16[136,1024]{1,0:T(8,128)(2,1)S(1)}, u32[]{:S(2)}, u32[]{:S(2)}) %collective-permute-start) | collective-permute-done | bytes 278560 | tf_op jit(solution)/shard_map/ppermute | solution.py:32
  10.4 0.1 pad_maximum_fusion.refs_0_
  10.4 7.1 %collective-permute-start.1 = (bf16[2,136,1024]{2,1,0:T(8,128)(2,1)S(1)}, bf16[2,136,1024]{2,1,0:T(8,128)(2,1)S(1)}, u32[]{:S(2)}, u32[]{:S(2)}) collective-permute-start(bf16[2,136,1024]{2,1,0:T(8,128)(2,1)S(1)} %pad_maximum_fusion.refs_0_), channel_id=1, source_target_pairs={{0,6},{2,4},{4,2},{6,0},{1,7},{3,5},{5,3},{7,1},{8,14},{10,12},{12... | collective-permute-start | bytes 1671176 | tf_op jit(solution)/shard_map/ppermute | solution.py:32
  17.6 0.0 copy-done
  17.6 0.6 broadcast_in_dim.23
  18.3 45.2 %all-to-all-start = ((bf16[8,8,1024]{2,1,0:T(8,128)(2,1)}), bf16[8,8,1024]{2,1,0:T(8,128)(2,1)S(1)}, u32[]{:S(2)}, u32[]{:S(2)}) async-start(bf16[8,8,1024]{2,1,0:T(8,128)(2,1)} %broadcast_in_dim.23), calls=%async_computation | async-start | bytes 262144 | tf_op jit(solution)/shard_map/all_to_all | solution.py:116
  63.4 4.0 %collective-permute-start.2 = (bf16[2,136,1024]{2,1,0:T(8,128)(2,1)S(1)}, bf16[2,136,1024]{2,1,0:T(8,128)(2,1)S(1)}, u32[]{:S(2)}, u32[]{:S(2)}) collective-permute-start(bf16[2,136,1024]{2,1,0:T(8,128)(2,1)S(1)} %pad_maximum_fusion.refs_0_), channel_id=1, source_target_pairs={{0,1},{1,0},{2,3},{3,2},{4,5},{5,4},{6,7},{7,6},{8,9},{9,8},{10,11... | collective-permute-start | bytes 1671176 | tf_op jit(solution)/shard_map/ppermute | solution.py:27
  67.4 0.0 collective-permute-done.1.refs_1_
  67.4 2.0 %collective-permute-start.3 = (bf16[2,136,1024]{2,1,0:T(8,128)(2,1)S(1)}, bf16[2,136,1024]{2,1,0:T(8,128)(2,1)S(1)}, u32[]{:S(2)}, u32[]{:S(2)}) collective-permute-start(bf16[2,136,1024]{2,1,0:T(8,128)(2,1)S(1)} %collective-permute-done.1.refs_1_), channel_id=1, source_target_pairs={{0,1},{1,0},{2,3},{3,2},{4,5},{5,4},{6,7},{7,6},{8,9},{9,8},{10,11... | collective-permute-start | bytes 1671176 | tf_op jit(solution)/shard_map/ppermute | solution.py:27
  69.3 11.2 %all-to-all-done.refs_4_ = bf16[8,8,1024]{2,1,0:T(8,128)(2,1)S(1)} async-done(((bf16[8,8,1024]{2,1,0:T(8,128)(2,1)}), bf16[8,8,1024]{2,1,0:T(8,128)(2,1)S(1)}, u32[]{:S(2)}, u32[]{:S(2)}) %all-to-all-start) | async-done | bytes 131104 | tf_op jit(solution)/shard_map/all_to_all | solution.py:116
  80.5 4.3 %collective-permute-start.6 = (bf16[8,8,1024]{2,1,0:T(8,128)(2,1)S(1)}, bf16[8,8,1024]{2,1,0:T(8,128)(2,1)S(1)}, u32[]{:S(2)}, u32[]{:S(2)}) collective-permute-start(bf16[8,8,1024]{2,1,0:T(8,128)(2,1)S(1)} %all-to-all-done.refs_4_), channel_id=1, source_target_pairs={{0,8},{8,16},{16,24},{24,32},{32,40},{40,48},{48,56},{56,64},{64,7... | collective-permute-start | bytes 393224 | tf_op jit(solution)/shard_map/ppermute | solution.py:27
  84.8 12.0 %collective-permute-start.5 = (bf16[8,8,1024]{2,1,0:T(8,128)(2,1)S(1)}, bf16[8,8,1024]{2,1,0:T(8,128)(2,1)S(1)}, u32[]{:S(2)}, u32[]{:S(2)}) collective-permute-start(bf16[8,8,1024]{2,1,0:T(8,128)(2,1)S(1)} %all-to-all-done.refs_4_), channel_id=1, source_target_pairs={{0,240},{8,24},{16,0},{24,40},{32,16},{40,56},{48,32},{56,72},{64,... | collective-permute-start | bytes 393224 | tf_op jit(solution)/shard_map/ppermute | solution.py:123
  96.8 2.0 %collective-permute-start.4 = (bf16[8,8,1024]{2,1,0:T(8,128)(2,1)S(1)}, bf16[8,8,1024]{2,1,0:T(8,128)(2,1)S(1)}, u32[]{:S(2)}, u32[]{:S(2)}) collective-permute-start(bf16[8,8,1024]{2,1,0:T(8,128)(2,1)S(1)} %all-to-all-done.refs_4_), channel_id=1, source_target_pairs={{0,248},{8,0},{16,8},{24,16},{32,24},{40,32},{48,40},{56,48},{64,5... | collective-permute-start | bytes 393224 | tf_op jit(solution)/shard_map/ppermute | solution.py:27
  98.8 0.0 collective-permute-done.2.refs_2_
  98.8 0.0 collective-permute-done.6.refs_7_
  98.8 0.0 collective-permute-done.5.refs_6_
  98.8 3.7 %collective-permute-done.4.refs_5_ = bf16[8,8,1024]{2,1,0:T(8,128)(2,1)S(1)} collective-permute-done((bf16[8,8,1024]{2,1,0:T(8,128)(2,1)S(1)}, bf16[8,8,1024]{2,1,0:T(8,128)(2,1)S(1)}, u32[]{:S(2)}, u32[]{:S(2)}) %collective-permute-start.4) | collective-permute-done | bytes 131104 | tf_op jit(solution)/shard_map/ppermute | solution.py:27
  102.6 0.0 collective-permute-done.3.refs_3_
  102.6 3.4 %scores.1 = f32[64,128]{1,0:T(8,128)} custom-call(s32[1]{0:T(128)} %bitcast.shift_ref, f32[1,128]{1,0:T(1,128)} %bitcast.16, bf16[2,136,1024]{2,1,0:T(8,128)(2,1)S(1)} %pad_maximum_fusion.refs_0_, bf16[2,136,1024]{2,1,0:T(8,128)(2,1)S(1)} %collective-permute-done.1.refs_1_, bf16[2,136,1024]{2,1,0:T(8,128)(2,1)S(1)} %collective-permute-done.2.refs_2_, ...), custom_call_target="tpu_custom_call" | custom-call | tf_op jit(solution)/shard_map/scores/pallas_call | solution.py:126
  105.9 29.0 %all_to_all.16 = f32[64,1,128]{2,1,0:T(1,128)S(1)} all-to-all(f32[64,1,128]{2,1,0:T(1,128)} %bitcast.15), channel_id=1, replica_groups={{128,160,192,224,0,32,64,96,136,168,200,232,8,40,72,104,144,176,208,240..., dimensions={0} | all-to-all | bytes 65536 | tf_op jit(solution)/shard_map/all_to_all | solution.py:150
  135.0 0.7 finish.1
  (1 shorter events, 0.0 us)
Async XLA Ops:
  0.6 16.9 %copy-start = (bf16[16,1024]{1,0:T(8,128)(2,1)S(1)}, bf16[16,1024]{1,0:T(8,128)(2,1)}, u32[]{:S(2)}) copy-start(bf16[16,1024]{1,0:T(8,128)(2,1)} %param.5) | copy-start | bytes 98308
  2.3 8.0 %collective-permute-start = (bf16[136,1024]{1,0:T(8,128)(2,1)S(1)}, bf16[136,1024]{1,0:T(8,128)(2,1)S(1)}, u32[]{:S(2)}, u32[]{:S(2)}) collective-permute-start(bf16[136,1024]{1,0:T(8,128)(2,1)S(1)} %get-tuple-element.7), channel_id=1, source_target_pairs={{0,2},{2,0},{4,6},{6,4},{1,3},{3,1},{5,7},{7,5},{8,10},{10,8},{12,... | collective-permute-start | bytes 835592 | tf_op jit(solution)/shard_map/ppermute | solution.py:32
  10.4 56.9 %collective-permute-start.1 = (bf16[2,136,1024]{2,1,0:T(8,128)(2,1)S(1)}, bf16[2,136,1024]{2,1,0:T(8,128)(2,1)S(1)}, u32[]{:S(2)}, u32[]{:S(2)}) collective-permute-start(bf16[2,136,1024]{2,1,0:T(8,128)(2,1)S(1)} %pad_maximum_fusion.refs_0_), channel_id=1, source_target_pairs={{0,6},{2,4},{4,2},{6,0},{1,7},{3,5},{5,3},{7,1},{8,14},{10,12},{12... | collective-permute-start | bytes 1671176 | tf_op jit(solution)/shard_map/ppermute | solution.py:32
  18.3 62.2 %all-to-all-start = ((bf16[8,8,1024]{2,1,0:T(8,128)(2,1)}), bf16[8,8,1024]{2,1,0:T(8,128)(2,1)S(1)}, u32[]{:S(2)}, u32[]{:S(2)}) async-start(bf16[8,8,1024]{2,1,0:T(8,128)(2,1)} %broadcast_in_dim.23), calls=%async_computation | async-start | bytes 262144 | tf_op jit(solution)/shard_map/all_to_all | solution.py:116
  63.4 35.4 %collective-permute-start.2 = (bf16[2,136,1024]{2,1,0:T(8,128)(2,1)S(1)}, bf16[2,136,1024]{2,1,0:T(8,128)(2,1)S(1)}, u32[]{:S(2)}, u32[]{:S(2)}) collective-permute-start(bf16[2,136,1024]{2,1,0:T(8,128)(2,1)S(1)} %pad_maximum_fusion.refs_0_), channel_id=1, source_target_pairs={{0,1},{1,0},{2,3},{3,2},{4,5},{5,4},{6,7},{7,6},{8,9},{9,8},{10,11... | collective-permute-start | bytes 1671176 | tf_op jit(solution)/shard_map/ppermute | solution.py:27
  67.4 35.2 %collective-permute-start.3 = (bf16[2,136,1024]{2,1,0:T(8,128)(2,1)S(1)}, bf16[2,136,1024]{2,1,0:T(8,128)(2,1)S(1)}, u32[]{:S(2)}, u32[]{:S(2)}) collective-permute-start(bf16[2,136,1024]{2,1,0:T(8,128)(2,1)S(1)} %collective-permute-done.1.refs_1_), channel_id=1, source_target_pairs={{0,1},{1,0},{2,3},{3,2},{4,5},{5,4},{6,7},{7,6},{8,9},{9,8},{10,11... | collective-permute-start | bytes 1671176 | tf_op jit(solution)/shard_map/ppermute | solution.py:27
  80.5 18.3 %collective-permute-start.6 = (bf16[8,8,1024]{2,1,0:T(8,128)(2,1)S(1)}, bf16[8,8,1024]{2,1,0:T(8,128)(2,1)S(1)}, u32[]{:S(2)}, u32[]{:S(2)}) collective-permute-start(bf16[8,8,1024]{2,1,0:T(8,128)(2,1)S(1)} %all-to-all-done.refs_4_), channel_id=1, source_target_pairs={{0,8},{8,16},{16,24},{24,32},{32,40},{40,48},{48,56},{56,64},{64,7... | collective-permute-start | bytes 393224 | tf_op jit(solution)/shard_map/ppermute | solution.py:27
  84.8 14.0 %collective-permute-start.5 = (bf16[8,8,1024]{2,1,0:T(8,128)(2,1)S(1)}, bf16[8,8,1024]{2,1,0:T(8,128)(2,1)S(1)}, u32[]{:S(2)}, u32[]{:S(2)}) collective-permute-start(bf16[8,8,1024]{2,1,0:T(8,128)(2,1)S(1)} %all-to-all-done.refs_4_), channel_id=1, source_target_pairs={{0,240},{8,24},{16,0},{24,40},{32,16},{40,56},{48,32},{56,72},{64,... | collective-permute-start | bytes 393224 | tf_op jit(solution)/shard_map/ppermute | solution.py:123
  96.8 5.7 %collective-permute-start.4 = (bf16[8,8,1024]{2,1,0:T(8,128)(2,1)S(1)}, bf16[8,8,1024]{2,1,0:T(8,128)(2,1)S(1)}, u32[]{:S(2)}, u32[]{:S(2)}) collective-permute-start(bf16[8,8,1024]{2,1,0:T(8,128)(2,1)S(1)} %all-to-all-done.refs_4_), channel_id=1, source_target_pairs={{0,248},{8,0},{16,8},{24,16},{32,24},{40,32},{48,40},{56,48},{64,5... | collective-permute-start | bytes 393224 | tf_op jit(solution)/shard_map/ppermute | solution.py:27

commit v4 on v3

--- a/solution.py
+++ b/solution.py
@@ -48,21 +48,25 @@
         at += size
     count = packs[0].shape[0] - 8
     docs = lax.broadcasted_iota(jnp.int32, (count, bias_ref.shape[1]), 1).astype(jnp.float32)
-    best = jnp.full((1, at), LOW, jnp.float32)
+    whole = jnp.concatenate([pack[:count, :] for pack in packs], axis=0)
+    sims_ref[...] = lax.dot_general(
+        whole, rows_ref[...], (((1,), (1,)), ((), ())), preferred_element_type=jnp.float32
+    ).reshape(sims_ref.shape)
     biases = []
+    best = jnp.full((8, at), LOW, jnp.float32)
     for k, pack in enumerate(packs):
         code = pack[count:, :128].astype(jnp.float32).T[:, :1]
         bias = jnp.sum(jnp.where(docs == code, bias_ref[...], 0.0), axis=1, keepdims=True)
         valid = code < float(bias_ref.shape[1])
         biases.append(jnp.where(valid, bias, -jnp.inf))
-        sim = lax.dot_general(
-            pack[:count, :], rows_ref[...], (((1,), (1,)), ((), ())), preferred_element_type=jnp.float32
-        )
-        sims_ref[k] = sim
-        best = jnp.maximum(best, jnp.max(jnp.where(valid, sim, LOW), axis=0, keepdims=True))
-    total = jnp.zeros((1, at), jnp.float32)
+        sim = jnp.where(valid, sims_ref[k], LOW)
+        best = jnp.maximum(best, jnp.max(sim.reshape(count // 8, 8, at), axis=0))
+    best = jnp.max(best, axis=0, keepdims=True)
+    total = jnp.zeros((8, at), jnp.float32)
     for k in range(len(packs)):
-        total += jnp.sum(jnp.exp(2.0 * (sims_ref[k] - best) + biases[k]), axis=0, keepdims=True)
+        term = jnp.exp(2.0 * (sims_ref[k] - best) + biases[k])
+        total += jnp.sum(term.reshape(count // 8, 8, at), axis=0)
+    total = jnp.sum(total, axis=0, keepdims=True)
     lane = lax.broadcasted_iota(jnp.int32, (rows, at), 1)
     line = lax.broadcasted_iota(jnp.int32, (rows, at), 0)
     per = 8 * LOOP
@@ -72,14 +76,8 @@
     query = lax.broadcasted_iota(jnp.int32, (at, 128), 0) % 8
     column = lax.broadcasted_iota(jnp.int32, (at, 128), 1)
     value = lax.dot_general(
-        jnp.where(mine, best, 0.0),
-        (query == column).astype(jnp.float32),
-        (((1,), (0,)), ((), ())),
-        precision=lax.Precision.HIGHEST,
-        preferred_element_type=jnp.float32,
-    ) + lax.dot_general(
-        jnp.where(mine, total, 0.0),
-        (query + 8 == column).astype(jnp.float32),
+        jnp.concatenate([jnp.where(mine, best, 0.0), jnp.where(mine, total, 0.0)], axis=1),
+        jnp.concatenate([query == column, query + 8 == column], axis=0).astype(jnp.float32),
         (((1,), (0,)), ((), ())),
         precision=lax.Precision.HIGHEST,
         preferred_element_type=jnp.float32,
@@ -106,18 +104,19 @@
     side = lax.axis_index("merge")
     place = lax.axis_index("ring")
     half = queries.shape[0] // 2
-    mine = lax.dynamic_slice_in_dim(queries, side * half, half, 0)
     code = jnp.where(span_valid == 1, span_doc, doc_bias.shape[0]).astype(jnp.bfloat16)
     codes = jnp.pad(code[None, :], ((0, 7), (0, spans.shape[1] - code.shape[0])))
     pack = jnp.concatenate([spans, codes], axis=0)
 
     loops = [[ring_place(r, i) for i in range(LOOP)] for r in range(RESIDUES)]
+    mine = lax.dynamic_slice_in_dim(queries, side * half, half, 0)
     copies = jnp.broadcast_to(mine[None], (LOOP, *mine.shape))
     near = lax.all_to_all(copies, "ring", 0, 0, axis_index_groups=loops, tiled=True)
     other = mirrored(pack, 1)
     two = jnp.stack([pack, other])
     four = [two, mirrored(two, 3)]
-    pairs = four + [shifted(one, "merge", 1) for one in four]
+    pairs = [*four, shifted(two, "merge", 1)]
+    pairs.append(shifted(four[1], "merge", 1))
     up = shifted(near, "ring", -1)
     down = shifted(near, "ring", 1)
     across = lax.ppermute(near, "ring", [(k, (k + 4 * (k % 2) - 2) % RING) for k in range(RING)])
@@ -125,7 +124,7 @@
     slots = RING * 2
     stats = pl.pallas_call(
         scores_kernel,
-        out_shape=jax.ShapeDtypeStruct((slots, 128), jnp.float32),
+        out_shape=pltpu.VMEM((slots, 128), jnp.float32),
         in_specs=[pl.BlockSpec(memory_space=pltpu.SMEM)] + [pl.BlockSpec(memory_space=pltpu.VMEM)] * 9,
         out_specs=pl.BlockSpec(memory_space=pltpu.VMEM),
         scratch_shapes=[

time: 136 us -> 135 us (level)
  no operation moved by 1% of the time
where the time goes in v4:
time: 135 us; the launch traced here: 134 us
  starting transfers between devices  80.6 us (60%)
  blocking collectives  28.9 us (21%)
  waiting for transfers between devices  18.8 us (14%)
  Pallas kernels  2.92 us (2%)
  other arithmetic  1.74 us (1%)
    all_to_all x1, starting transfers between devices, shards(): lax.all_to_all(copies, 'ring', 0, 0, axis_index_groups=loops, tiled=True)  45.2 us
    all_to_all x1, blocking collectives, shards(): lax.all_to_all(stats, GROUP, 0, 0, axis_index_groups=columns, tiled=True)  28.9 us
    ppermute x4, starting transfers between devices, shifted(): lax.ppermute(value, axis, [(k, (k + by) % size) for k in range(size)])  12.1 us
    ppermute x1, starting transfers between devices, shards(): lax.ppermute(near, 'ring', [(k, (k + 4 * (k % 2) - 2) % RING) for k in ra...  12 us
    ppermute x2, starting transfers between devices, mirrored(): return lax.ppermute(value, 'row', [(k, k ^ mask) for k in range(size)])  11.2 us
    all_to_all x1, waiting for transfers between devices, shards(): lax.all_to_all(copies, 'ring', 0, 0, axis_index_groups=loops, tiled=True)  11.2 us
    ppermute x2, waiting for transfers between devices, mirrored(): return lax.ppermute(value, 'row', [(k, k ^ mask) for k in range(size)])  3.92 us
    ppermute x4, waiting for transfers between devices, shifted(): lax.ppermute(value, axis, [(k, (k + by) % size) for k in range(size)])  3.75 us
  transfers between devices with their start and end apart: 8, of which 3 were waited for; matrix products, arithmetic and copies ran while one was open for 0% of the time, Pallas kernels for 0%

profile of v4, /device:TPU:33, one launch (start us, length us, event | category | flops | bytes accessed | tf_op | source)
XLA Modules:
  0.0 134.4 jit_solution(12636943809472773645)
XLA Ops:
  0.6 0.0 copy-start
  0.6 0.7 fusion.3
  1.3 1.0 fusion.4
  2.3 4.1 %collective-permute-start = (bf16[136,1024]{1,0:T(8,128)(2,1)S(1)}, bf16[136,1024]{1,0:T(8,128)(2,1)S(1)}, u32[]{:S(2)}, u32[]{:S(2)}) collective-permute-start(bf16[136,1024]{1,0:T(8,128)(2,1)S(1)} %get-tuple-element.7), channel_id=1, source_target_pairs={{0,2},{2,0},{4,6},{6,4},{1,3},{3,1},{5,7},{7,5},{8,10},{10,8},{12,... | collective-permute-start | bytes 835592 | tf_op jit(solution)/shard_map/ppermute | solution.py:32
  6.5 3.9 %collective-permute-done = bf16[136,1024]{1,0:T(8,128)(2,1)S(1)} collective-permute-done((bf16[136,1024]{1,0:T(8,128)(2,1)S(1)}, bf16[136,1024]{1,0:T(8,128)(2,1)S(1)}, u32[]{:S(2)}, u32[]{:S(2)}) %collective-permute-start) | collective-permute-done | bytes 278560 | tf_op jit(solution)/shard_map/ppermute | solution.py:32
  10.4 0.1 pad_maximum_fusion.refs_0_
  10.4 7.1 %collective-permute-start.1 = (bf16[2,136,1024]{2,1,0:T(8,128)(2,1)S(1)}, bf16[2,136,1024]{2,1,0:T(8,128)(2,1)S(1)}, u32[]{:S(2)}, u32[]{:S(2)}) collective-permute-start(bf16[2,136,1024]{2,1,0:T(8,128)(2,1)S(1)} %pad_maximum_fusion.refs_0_), channel_id=1, source_target_pairs={{0,6},{2,4},{4,2},{6,0},{1,7},{3,5},{5,3},{7,1},{8,14},{10,12},{12... | collective-permute-start | bytes 1671176 | tf_op jit(solution)/shard_map/ppermute | solution.py:32
  17.6 0.0 copy-done
  17.6 0.6 broadcast_in_dim.23
  18.3 45.2 %all-to-all-start = ((bf16[8,8,1024]{2,1,0:T(8,128)(2,1)}), bf16[8,8,1024]{2,1,0:T(8,128)(2,1)S(1)}, u32[]{:S(2)}, u32[]{:S(2)}) async-start(bf16[8,8,1024]{2,1,0:T(8,128)(2,1)} %broadcast_in_dim.23), calls=%async_computation | async-start | bytes 262144 | tf_op jit(solution)/shard_map/all_to_all | solution.py:114
  63.4 4.0 %collective-permute-start.2 = (bf16[2,136,1024]{2,1,0:T(8,128)(2,1)S(1)}, bf16[2,136,1024]{2,1,0:T(8,128)(2,1)S(1)}, u32[]{:S(2)}, u32[]{:S(2)}) collective-permute-start(bf16[2,136,1024]{2,1,0:T(8,128)(2,1)S(1)} %pad_maximum_fusion.refs_0_), channel_id=1, source_target_pairs={{0,1},{1,0},{2,3},{3,2},{4,5},{5,4},{6,7},{7,6},{8,9},{9,8},{10,11... | collective-permute-start | bytes 1671176 | tf_op jit(solution)/shard_map/ppermute | solution.py:27
  67.4 0.0 collective-permute-done.1.refs_1_
  67.4 2.0 %collective-permute-start.3 = (bf16[2,136,1024]{2,1,0:T(8,128)(2,1)S(1)}, bf16[2,136,1024]{2,1,0:T(8,128)(2,1)S(1)}, u32[]{:S(2)}, u32[]{:S(2)}) collective-permute-start(bf16[2,136,1024]{2,1,0:T(8,128)(2,1)S(1)} %collective-permute-done.1.refs_1_), channel_id=1, source_target_pairs={{0,1},{1,0},{2,3},{3,2},{4,5},{5,4},{6,7},{7,6},{8,9},{9,8},{10,11... | collective-permute-start | bytes 1671176 | tf_op jit(solution)/shard_map/ppermute | solution.py:27
  69.3 11.2 %all-to-all-done.refs_4_ = bf16[8,8,1024]{2,1,0:T(8,128)(2,1)S(1)} async-done(((bf16[8,8,1024]{2,1,0:T(8,128)(2,1)}), bf16[8,8,1024]{2,1,0:T(8,128)(2,1)S(1)}, u32[]{:S(2)}, u32[]{:S(2)}) %all-to-all-start) | async-done | bytes 131104 | tf_op jit(solution)/shard_map/all_to_all | solution.py:114
  80.5 4.3 %collective-permute-start.6 = (bf16[8,8,1024]{2,1,0:T(8,128)(2,1)S(1)}, bf16[8,8,1024]{2,1,0:T(8,128)(2,1)S(1)}, u32[]{:S(2)}, u32[]{:S(2)}) collective-permute-start(bf16[8,8,1024]{2,1,0:T(8,128)(2,1)S(1)} %all-to-all-done.refs_4_), channel_id=1, source_target_pairs={{0,8},{8,16},{16,24},{24,32},{32,40},{40,48},{48,56},{56,64},{64,7... | collective-permute-start | bytes 393224 | tf_op jit(solution)/shard_map/ppermute | solution.py:27
  84.8 12.0 %collective-permute-start.5 = (bf16[8,8,1024]{2,1,0:T(8,128)(2,1)S(1)}, bf16[8,8,1024]{2,1,0:T(8,128)(2,1)S(1)}, u32[]{:S(2)}, u32[]{:S(2)}) collective-permute-start(bf16[8,8,1024]{2,1,0:T(8,128)(2,1)S(1)} %all-to-all-done.refs_4_), channel_id=1, source_target_pairs={{0,240},{8,24},{16,0},{24,40},{32,16},{40,56},{48,32},{56,72},{64,... | collective-permute-start | bytes 393224 | tf_op jit(solution)/shard_map/ppermute | solution.py:122
  96.8 2.0 %collective-permute-start.4 = (bf16[8,8,1024]{2,1,0:T(8,128)(2,1)S(1)}, bf16[8,8,1024]{2,1,0:T(8,128)(2,1)S(1)}, u32[]{:S(2)}, u32[]{:S(2)}) collective-permute-start(bf16[8,8,1024]{2,1,0:T(8,128)(2,1)S(1)} %all-to-all-done.refs_4_), channel_id=1, source_target_pairs={{0,248},{8,0},{16,8},{24,16},{32,24},{40,32},{48,40},{56,48},{64,5... | collective-permute-start | bytes 393224 | tf_op jit(solution)/shard_map/ppermute | solution.py:27
  98.8 0.0 collective-permute-done.2.refs_2_
  98.8 0.0 collective-permute-done.6.refs_7_
  98.8 0.0 collective-permute-done.5.refs_6_
  98.8 3.7 %collective-permute-done.4.refs_5_ = bf16[8,8,1024]{2,1,0:T(8,128)(2,1)S(1)} collective-permute-done((bf16[8,8,1024]{2,1,0:T(8,128)(2,1)S(1)}, bf16[8,8,1024]{2,1,0:T(8,128)(2,1)S(1)}, u32[]{:S(2)}, u32[]{:S(2)}) %collective-permute-start.4) | collective-permute-done | bytes 131104 | tf_op jit(solution)/shard_map/ppermute | solution.py:27
  102.6 0.0 collective-permute-done.3.refs_3_
  102.6 2.3 %scores.1 = f32[64,128]{1,0:T(8,128)S(1)} custom-call(s32[1]{0:T(128)} %bitcast.shift_ref, f32[1,128]{1,0:T(1,128)} %bitcast.16, bf16[2,136,1024]{2,1,0:T(8,128)(2,1)S(1)} %pad_maximum_fusion.refs_0_, bf16[2,136,1024]{2,1,0:T(8,128)(2,1)S(1)} %collective-permute-done.1.refs_1_, bf16[2,136,1024]{2,1,0:T(8,128)(2,1)S(1)} %collective-permute-done.2.refs_2_, ...), custom_call_target="tpu_custom_call" | custom-call | tf_op jit(solution)/shard_map/scores/pallas_call | solution.py:125
  104.8 28.9 %all_to_all.16 = f32[64,1,128]{2,1,0:T(1,128)S(1)} all-to-all(f32[64,1,128]{2,1,0:T(1,128)S(1)} %bitcast.13), channel_id=1, replica_groups={{128,160,192,224,0,32,64,96,136,168,200,232,8,40,72,104,144,176,208,240..., dimensions={0} | all-to-all | bytes 65536 | tf_op jit(solution)/shard_map/all_to_all | solution.py:149
  133.7 0.7 finish.1
  (1 shorter events, 0.0 us)
Async XLA Ops:
  0.6 16.9 %copy-start = (bf16[16,1024]{1,0:T(8,128)(2,1)S(1)}, bf16[16,1024]{1,0:T(8,128)(2,1)}, u32[]{:S(2)}) copy-start(bf16[16,1024]{1,0:T(8,128)(2,1)} %param.5) | copy-start | bytes 98308
  2.3 8.0 %collective-permute-start = (bf16[136,1024]{1,0:T(8,128)(2,1)S(1)}, bf16[136,1024]{1,0:T(8,128)(2,1)S(1)}, u32[]{:S(2)}, u32[]{:S(2)}) collective-permute-start(bf16[136,1024]{1,0:T(8,128)(2,1)S(1)} %get-tuple-element.7), channel_id=1, source_target_pairs={{0,2},{2,0},{4,6},{6,4},{1,3},{3,1},{5,7},{7,5},{8,10},{10,8},{12,... | collective-permute-start | bytes 835592 | tf_op jit(solution)/shard_map/ppermute | solution.py:32
  10.4 56.9 %collective-permute-start.1 = (bf16[2,136,1024]{2,1,0:T(8,128)(2,1)S(1)}, bf16[2,136,1024]{2,1,0:T(8,128)(2,1)S(1)}, u32[]{:S(2)}, u32[]{:S(2)}) collective-permute-start(bf16[2,136,1024]{2,1,0:T(8,128)(2,1)S(1)} %pad_maximum_fusion.refs_0_), channel_id=1, source_target_pairs={{0,6},{2,4},{4,2},{6,0},{1,7},{3,5},{5,3},{7,1},{8,14},{10,12},{12... | collective-permute-start | bytes 1671176 | tf_op jit(solution)/shard_map/ppermute | solution.py:32
  18.3 62.2 %all-to-all-start = ((bf16[8,8,1024]{2,1,0:T(8,128)(2,1)}), bf16[8,8,1024]{2,1,0:T(8,128)(2,1)S(1)}, u32[]{:S(2)}, u32[]{:S(2)}) async-start(bf16[8,8,1024]{2,1,0:T(8,128)(2,1)} %broadcast_in_dim.23), calls=%async_computation | async-start | bytes 262144 | tf_op jit(solution)/shard_map/all_to_all | solution.py:114
  63.4 35.4 %collective-permute-start.2 = (bf16[2,136,1024]{2,1,0:T(8,128)(2,1)S(1)}, bf16[2,136,1024]{2,1,0:T(8,128)(2,1)S(1)}, u32[]{:S(2)}, u32[]{:S(2)}) collective-permute-start(bf16[2,136,1024]{2,1,0:T(8,128)(2,1)S(1)} %pad_maximum_fusion.refs_0_), channel_id=1, source_target_pairs={{0,1},{1,0},{2,3},{3,2},{4,5},{5,4},{6,7},{7,6},{8,9},{9,8},{10,11... | collective-permute-start | bytes 1671176 | tf_op jit(solution)/shard_map/ppermute | solution.py:27
  67.4 35.2 %collective-permute-start.3 = (bf16[2,136,1024]{2,1,0:T(8,128)(2,1)S(1)}, bf16[2,136,1024]{2,1,0:T(8,128)(2,1)S(1)}, u32[]{:S(2)}, u32[]{:S(2)}) collective-permute-start(bf16[2,136,1024]{2,1,0:T(8,128)(2,1)S(1)} %collective-permute-done.1.refs_1_), channel_id=1, source_target_pairs={{0,1},{1,0},{2,3},{3,2},{4,5},{5,4},{6,7},{7,6},{8,9},{9,8},{10,11... | collective-permute-start | bytes 1671176 | tf_op jit(solution)/shard_map/ppermute | solution.py:27
  80.5 18.3 %collective-permute-start.6 = (bf16[8,8,1024]{2,1,0:T(8,128)(2,1)S(1)}, bf16[8,8,1024]{2,1,0:T(8,128)(2,1)S(1)}, u32[]{:S(2)}, u32[]{:S(2)}) collective-permute-start(bf16[8,8,1024]{2,1,0:T(8,128)(2,1)S(1)} %all-to-all-done.refs_4_), channel_id=1, source_target_pairs={{0,8},{8,16},{16,24},{24,32},{32,40},{40,48},{48,56},{56,64},{64,7... | collective-permute-start | bytes 393224 | tf_op jit(solution)/shard_map/ppermute | solution.py:27
  84.8 14.0 %collective-permute-start.5 = (bf16[8,8,1024]{2,1,0:T(8,128)(2,1)S(1)}, bf16[8,8,1024]{2,1,0:T(8,128)(2,1)S(1)}, u32[]{:S(2)}, u32[]{:S(2)}) collective-permute-start(bf16[8,8,1024]{2,1,0:T(8,128)(2,1)S(1)} %all-to-all-done.refs_4_), channel_id=1, source_target_pairs={{0,240},{8,24},{16,0},{24,40},{32,16},{40,56},{48,32},{56,72},{64,... | collective-permute-start | bytes 393224 | tf_op jit(solution)/shard_map/ppermute | solution.py:122
  96.8 5.7 %collective-permute-start.4 = (bf16[8,8,1024]{2,1,0:T(8,128)(2,1)S(1)}, bf16[8,8,1024]{2,1,0:T(8,128)(2,1)S(1)}, u32[]{:S(2)}, u32[]{:S(2)}) collective-permute-start(bf16[8,8,1024]{2,1,0:T(8,128)(2,1)S(1)} %all-to-all-done.refs_4_), channel_id=1, source_target_pairs={{0,248},{8,0},{16,8},{24,16},{32,24},{40,32},{48,40},{56,48},{64,5... | collective-permute-start | bytes 393224 | tf_op jit(solution)/shard_map/ppermute | solution.py:27

commit v5 on v4

--- a/solution.py
+++ b/solution.py
@@ -11,15 +11,15 @@
 ROW = 4
 RESIDUES = 4
 LOOP = RING // RESIDUES
-FIRST = RING - RESIDUES
-LAST = RING // 2
+FIRST = RING - 2 * RESIDUES
+TURN = 3 * LOOP // 4
 LOW = -1e30
 
 GROUP = ("ring", "row", "merge")
 
 
-def ring_place(residue, step, start=FIRST):
-    return (start + RESIDUES * step + residue) % RING
+def ring_place(residue, step):
+    return (FIRST + RESIDUES * step + residue) % RING
 
 
 def shifted(value, axis, by):
@@ -70,8 +70,7 @@
     lane = lax.broadcasted_iota(jnp.int32, (rows, at), 1)
     line = lax.broadcasted_iota(jnp.int32, (rows, at), 0)
     per = 8 * LOOP
-    turn = (LAST - FIRST) // RESIDUES
-    slot = ((lane // per + shift_ref[0]) % RESIDUES) * LOOP + (lane // 8 + LOOP - turn) % LOOP
+    slot = ((lane // per + shift_ref[0]) % RESIDUES) * LOOP + (lane // 8 + LOOP - TURN) % LOOP
     mine = slot == line
     query = lax.broadcasted_iota(jnp.int32, (at, 128), 0) % 8
     column = lax.broadcasted_iota(jnp.int32, (at, 128), 1)
@@ -117,10 +116,9 @@
     four = [two, mirrored(two, 3)]
     pairs = [*four, shifted(two, "merge", 1)]
     pairs.append(shifted(four[1], "merge", 1))
+    across = shifted(near, "ring", 2)
+    down = shifted(near, "ring", 1)
     up = shifted(near, "ring", -1)
-    down = shifted(near, "ring", 1)
-    across = lax.ppermute(near, "ring", [(k, (k + 4 * (k % 2) - 2) % RING) for k in range(RING)])
-
     slots = RING * 2
     stats = pl.pallas_call(
         scores_kernel,
@@ -133,13 +131,13 @@
         ],
         name="scores",
     )(
-        (place % RESIDUES).astype(jnp.int32)[None],
+        ((place + RING - FIRST) % RESIDUES).astype(jnp.int32)[None],
         doc_bias[None, :],
         *[in_vmem(pair) for pair in pairs],
         *[in_vmem(piece) for piece in (near, up, across, down)],
     )
     owners = [
-        (ring_place(r, i, LAST) * ROW + x) * 2 + m
+        (ring_place(r, i + TURN) * ROW + x) * 2 + m
         for x in range(ROW)
         for m in range(2)
         for r in range(RESIDUES)

time: 135 us -> 132 us (0.978)
  waiting for transfers between devices: 18.8 us -> 13.7 us
  blocking collectives: 28.9 us -> 31.4 us
    ppermute x1 -> x0, starting transfers between devices: 12 us -> none  [shards(): lax.ppermute(near, 'ring', [(k, (k + 4 * (k % 2) - 2) % RING) for k in ra...]
    ppermute x4 -> x5, starting transfers between devices: 12.1 us -> 21 us  [shifted(): lax.ppermute(value, axis, [(k, (k + by) % size) for k in range(size)])]
    all_to_all x1, waiting for transfers between devices: 11.2 us -> 5.84 us  [shards(): lax.all_to_all(copies, 'ring', 0, 0, axis_index_groups=loops, tiled=True)]
    all_to_all x1, starting transfers between devices: 45.2 us -> 48.2 us  [shards(): lax.all_to_all(copies, 'ring', 0, 0, axis_index_groups=loops, tiled=True)]
    all_to_all x1, blocking collectives: 28.9 us -> 31.4 us  [shards(): lax.all_to_all(stats, GROUP, 0, 0, axis_index_groups=columns, tiled=True)]
    ppermute x4 -> x5, waiting for transfers between devices: 3.75 us -> 3.99 us  [shifted(): lax.ppermute(value, axis, [(k, (k + by) % size) for k in range(size)])]
  transfers between devices with their start and end apart: 8 -> 8, of which waited for: 3 -> 4; matrix products, arithmetic and copies ran while one was open for 0% -> 0% of each run, Pallas kernels for 0% -> 0%
where the time goes in v5:
time: 132 us
  starting transfers between devices  80.5 us (61%)
  blocking collectives  31.4 us (24%)
  waiting for transfers between devices  13.7 us (10%)
  Pallas kernels  2.92 us (2%)
  other arithmetic  1.74 us (1%)
    all_to_all x1, starting transfers between devices, shards(): lax.all_to_all(copies, 'ring', 0, 0, axis_index_groups=loops, tiled=True)  48.2 us
    all_to_all x1, blocking collectives, shards(): lax.all_to_all(stats, GROUP, 0, 0, axis_index_groups=columns, tiled=True)  31.4 us
    ppermute x5, starting transfers between devices, shifted(): lax.ppermute(value, axis, [(k, (k + by) % size) for k in range(size)])  21 us
    ppermute x2, starting transfers between devices, mirrored(): return lax.ppermute(value, 'row', [(k, k ^ mask) for k in range(size)])  11.2 us
    all_to_all x1, waiting for transfers between devices, shards(): lax.all_to_all(copies, 'ring', 0, 0, axis_index_groups=loops, tiled=True)  5.84 us
    ppermute x5, waiting for transfers between devices, shifted(): lax.ppermute(value, axis, [(k, (k + by) % size) for k in range(size)])  3.99 us
    ppermute x2, waiting for transfers between devices, mirrored(): return lax.ppermute(value, 'row', [(k, k ^ mask) for k in range(size)])  3.92 us
  transfers between devices with their start and end apart: 8, of which 4 were waited for; matrix products, arithmetic and copies ran while one was open for 0% of the time, Pallas kernels for 0%

profile of v5, /device:TPU:33, one launch (start us, length us, event | category | flops | bytes accessed | tf_op | source)
XLA Modules:
  0.0 131.8 jit_solution(6409323678594146453)
XLA Ops:
  0.6 0.0 copy-start
  0.6 0.7 fusion.3
  1.3 1.0 fusion.4
  2.3 4.1 %collective-permute-start = (bf16[136,1024]{1,0:T(8,128)(2,1)S(1)}, bf16[136,1024]{1,0:T(8,128)(2,1)S(1)}, u32[]{:S(2)}, u32[]{:S(2)}) collective-permute-start(bf16[136,1024]{1,0:T(8,128)(2,1)S(1)} %get-tuple-element.7), channel_id=1, source_target_pairs={{0,2},{2,0},{4,6},{6,4},{1,3},{3,1},{5,7},{7,5},{8,10},{10,8},{12,... | collective-permute-start | bytes 835592 | tf_op jit(solution)/shard_map/ppermute | solution.py:32
  6.5 3.9 %collective-permute-done = bf16[136,1024]{1,0:T(8,128)(2,1)S(1)} collective-permute-done((bf16[136,1024]{1,0:T(8,128)(2,1)S(1)}, bf16[136,1024]{1,0:T(8,128)(2,1)S(1)}, u32[]{:S(2)}, u32[]{:S(2)}) %collective-permute-start) | collective-permute-done | bytes 278560 | tf_op jit(solution)/shard_map/ppermute | solution.py:32
  10.4 0.1 pad_maximum_fusion.refs_0_
  10.4 7.1 %collective-permute-start.1 = (bf16[2,136,1024]{2,1,0:T(8,128)(2,1)S(1)}, bf16[2,136,1024]{2,1,0:T(8,128)(2,1)S(1)}, u32[]{:S(2)}, u32[]{:S(2)}) collective-permute-start(bf16[2,136,1024]{2,1,0:T(8,128)(2,1)S(1)} %pad_maximum_fusion.refs_0_), channel_id=1, source_target_pairs={{0,6},{2,4},{4,2},{6,0},{1,7},{3,5},{5,3},{7,1},{8,14},{10,12},{12... | collective-permute-start | bytes 1671176 | tf_op jit(solution)/shard_map/ppermute | solution.py:32
  17.6 0.0 copy-done
  17.6 0.6 broadcast_in_dim.23
  18.3 48.2 %all-to-all-start = ((bf16[8,8,1024]{2,1,0:T(8,128)(2,1)}), bf16[8,8,1024]{2,1,0:T(8,128)(2,1)S(1)}, u32[]{:S(2)}, u32[]{:S(2)}) async-start(bf16[8,8,1024]{2,1,0:T(8,128)(2,1)} %broadcast_in_dim.23), calls=%async_computation | async-start | bytes 262144 | tf_op jit(solution)/shard_map/all_to_all | solution.py:113
  66.5 4.2 %collective-permute-start.2 = (bf16[2,136,1024]{2,1,0:T(8,128)(2,1)S(1)}, bf16[2,136,1024]{2,1,0:T(8,128)(2,1)S(1)}, u32[]{:S(2)}, u32[]{:S(2)}) collective-permute-start(bf16[2,136,1024]{2,1,0:T(8,128)(2,1)S(1)} %pad_maximum_fusion.refs_0_), channel_id=1, source_target_pairs={{0,1},{1,0},{2,3},{3,2},{4,5},{5,4},{6,7},{7,6},{8,9},{9,8},{10,11... | collective-permute-start | bytes 1671176 | tf_op jit(solution)/shard_map/ppermute | solution.py:27
  70.7 0.0 collective-permute-done.1.refs_1_
  70.8 2.0 %collective-permute-start.3 = (bf16[2,136,1024]{2,1,0:T(8,128)(2,1)S(1)}, bf16[2,136,1024]{2,1,0:T(8,128)(2,1)S(1)}, u32[]{:S(2)}, u32[]{:S(2)}) collective-permute-start(bf16[2,136,1024]{2,1,0:T(8,128)(2,1)S(1)} %collective-permute-done.1.refs_1_), channel_id=1, source_target_pairs={{0,1},{1,0},{2,3},{3,2},{4,5},{5,4},{6,7},{7,6},{8,9},{9,8},{10,11... | collective-permute-start | bytes 1671176 | tf_op jit(solution)/shard_map/ppermute | solution.py:27
  72.7 5.8 %all-to-all-done.refs_4_ = bf16[8,8,1024]{2,1,0:T(8,128)(2,1)S(1)} async-done(((bf16[8,8,1024]{2,1,0:T(8,128)(2,1)}), bf16[8,8,1024]{2,1,0:T(8,128)(2,1)S(1)}, u32[]{:S(2)}, u32[]{:S(2)}) %all-to-all-start) | async-done | bytes 131104 | tf_op jit(solution)/shard_map/all_to_all | solution.py:113
  78.6 7.9 %collective-permute-start.6 = (bf16[8,8,1024]{2,1,0:T(8,128)(2,1)S(1)}, bf16[8,8,1024]{2,1,0:T(8,128)(2,1)S(1)}, u32[]{:S(2)}, u32[]{:S(2)}) collective-permute-start(bf16[8,8,1024]{2,1,0:T(8,128)(2,1)S(1)} %all-to-all-done.refs_4_), channel_id=1, source_target_pairs={{0,8},{8,16},{16,24},{24,32},{32,40},{40,48},{48,56},{56,64},{64,7... | collective-permute-start | bytes 393224 | tf_op jit(solution)/shard_map/ppermute | solution.py:27
  86.4 4.9 %collective-permute-start.5 = (bf16[8,8,1024]{2,1,0:T(8,128)(2,1)S(1)}, bf16[8,8,1024]{2,1,0:T(8,128)(2,1)S(1)}, u32[]{:S(2)}, u32[]{:S(2)}) collective-permute-start(bf16[8,8,1024]{2,1,0:T(8,128)(2,1)S(1)} %all-to-all-done.refs_4_), channel_id=1, source_target_pairs={{0,16},{8,24},{16,32},{24,40},{32,48},{40,56},{48,64},{56,72},{64,... | collective-permute-start | bytes 393224 | tf_op jit(solution)/shard_map/ppermute | solution.py:27
  91.4 2.0 %collective-permute-start.4 = (bf16[8,8,1024]{2,1,0:T(8,128)(2,1)S(1)}, bf16[8,8,1024]{2,1,0:T(8,128)(2,1)S(1)}, u32[]{:S(2)}, u32[]{:S(2)}) collective-permute-start(bf16[8,8,1024]{2,1,0:T(8,128)(2,1)S(1)} %all-to-all-done.refs_4_), channel_id=1, source_target_pairs={{0,248},{8,0},{16,8},{24,16},{32,24},{40,32},{48,40},{56,48},{64,5... | collective-permute-start | bytes 393224 | tf_op jit(solution)/shard_map/ppermute | solution.py:27
  93.4 0.0 collective-permute-done.2.refs_2_
  93.4 0.0 collective-permute-done.6.refs_7_
  93.4 2.9 %collective-permute-done.5.refs_6_ = bf16[8,8,1024]{2,1,0:T(8,128)(2,1)S(1)} collective-permute-done((bf16[8,8,1024]{2,1,0:T(8,128)(2,1)S(1)}, bf16[8,8,1024]{2,1,0:T(8,128)(2,1)S(1)}, u32[]{:S(2)}, u32[]{:S(2)}) %collective-permute-start.5) | collective-permute-done | bytes 131104 | tf_op jit(solution)/shard_map/ppermute | solution.py:27
  96.4 1.1 collective-permute-done.4.refs_5_
  97.4 0.0 collective-permute-done.3.refs_3_
  97.4 2.3 %scores.1 = f32[64,128]{1,0:T(8,128)S(1)} custom-call(s32[1]{0:T(128)} %bitcast.shift_ref, f32[1,128]{1,0:T(1,128)} %bitcast.16, bf16[2,136,1024]{2,1,0:T(8,128)(2,1)S(1)} %pad_maximum_fusion.refs_0_, bf16[2,136,1024]{2,1,0:T(8,128)(2,1)S(1)} %collective-permute-done.1.refs_1_, bf16[2,136,1024]{2,1,0:T(8,128)(2,1)S(1)} %collective-permute-done.2.refs_2_, ...), custom_call_target="tpu_custom_call" | custom-call | tf_op jit(solution)/shard_map/scores/pallas_call | solution.py:123
  99.7 31.4 %all_to_all.16 = f32[64,1,128]{2,1,0:T(1,128)S(1)} all-to-all(f32[64,1,128]{2,1,0:T(1,128)S(1)} %bitcast.13), channel_id=1, replica_groups={{128,160,192,224,0,32,64,96,136,168,200,232,8,40,72,104,144,176,208,240..., dimensions={0} | all-to-all | bytes 65536 | tf_op jit(solution)/shard_map/all_to_all | solution.py:147
  131.1 0.7 finish.1
  (1 shorter events, 0.0 us)
Async XLA Ops:
  0.6 16.9 %copy-start = (bf16[16,1024]{1,0:T(8,128)(2,1)S(1)}, bf16[16,1024]{1,0:T(8,128)(2,1)}, u32[]{:S(2)}) copy-start(bf16[16,1024]{1,0:T(8,128)(2,1)} %param.5) | copy-start | bytes 98308
  2.3 8.0 %collective-permute-start = (bf16[136,1024]{1,0:T(8,128)(2,1)S(1)}, bf16[136,1024]{1,0:T(8,128)(2,1)S(1)}, u32[]{:S(2)}, u32[]{:S(2)}) collective-permute-start(bf16[136,1024]{1,0:T(8,128)(2,1)S(1)} %get-tuple-element.7), channel_id=1, source_target_pairs={{0,2},{2,0},{4,6},{6,4},{1,3},{3,1},{5,7},{7,5},{8,10},{10,8},{12,... | collective-permute-start | bytes 835592 | tf_op jit(solution)/shard_map/ppermute | solution.py:32
  10.4 60.3 %collective-permute-start.1 = (bf16[2,136,1024]{2,1,0:T(8,128)(2,1)S(1)}, bf16[2,136,1024]{2,1,0:T(8,128)(2,1)S(1)}, u32[]{:S(2)}, u32[]{:S(2)}) collective-permute-start(bf16[2,136,1024]{2,1,0:T(8,128)(2,1)S(1)} %pad_maximum_fusion.refs_0_), channel_id=1, source_target_pairs={{0,6},{2,4},{4,2},{6,0},{1,7},{3,5},{5,3},{7,1},{8,14},{10,12},{12... | collective-permute-start | bytes 1671176 | tf_op jit(solution)/shard_map/ppermute | solution.py:32
  18.3 60.3 %all-to-all-start = ((bf16[8,8,1024]{2,1,0:T(8,128)(2,1)}), bf16[8,8,1024]{2,1,0:T(8,128)(2,1)S(1)}, u32[]{:S(2)}, u32[]{:S(2)}) async-start(bf16[8,8,1024]{2,1,0:T(8,128)(2,1)} %broadcast_in_dim.23), calls=%async_computation | async-start | bytes 262144 | tf_op jit(solution)/shard_map/all_to_all | solution.py:113
  66.5 26.9 %collective-permute-start.2 = (bf16[2,136,1024]{2,1,0:T(8,128)(2,1)S(1)}, bf16[2,136,1024]{2,1,0:T(8,128)(2,1)S(1)}, u32[]{:S(2)}, u32[]{:S(2)}) collective-permute-start(bf16[2,136,1024]{2,1,0:T(8,128)(2,1)S(1)} %pad_maximum_fusion.refs_0_), channel_id=1, source_target_pairs={{0,1},{1,0},{2,3},{3,2},{4,5},{5,4},{6,7},{7,6},{8,9},{9,8},{10,11... | collective-permute-start | bytes 1671176 | tf_op jit(solution)/shard_map/ppermute | solution.py:27
  70.8 26.7 %collective-permute-start.3 = (bf16[2,136,1024]{2,1,0:T(8,128)(2,1)S(1)}, bf16[2,136,1024]{2,1,0:T(8,128)(2,1)S(1)}, u32[]{:S(2)}, u32[]{:S(2)}) collective-permute-start(bf16[2,136,1024]{2,1,0:T(8,128)(2,1)S(1)} %collective-permute-done.1.refs_1_), channel_id=1, source_target_pairs={{0,1},{1,0},{2,3},{3,2},{4,5},{5,4},{6,7},{7,6},{8,9},{9,8},{10,11... | collective-permute-start | bytes 1671176 | tf_op jit(solution)/shard_map/ppermute | solution.py:27
  78.6 14.9 %collective-permute-start.6 = (bf16[8,8,1024]{2,1,0:T(8,128)(2,1)S(1)}, bf16[8,8,1024]{2,1,0:T(8,128)(2,1)S(1)}, u32[]{:S(2)}, u32[]{:S(2)}) collective-permute-start(bf16[8,8,1024]{2,1,0:T(8,128)(2,1)S(1)} %all-to-all-done.refs_4_), channel_id=1, source_target_pairs={{0,8},{8,16},{16,24},{24,32},{32,40},{40,48},{48,56},{56,64},{64,7... | collective-permute-start | bytes 393224 | tf_op jit(solution)/shard_map/ppermute | solution.py:27
  86.4 9.9 %collective-permute-start.5 = (bf16[8,8,1024]{2,1,0:T(8,128)(2,1)S(1)}, bf16[8,8,1024]{2,1,0:T(8,128)(2,1)S(1)}, u32[]{:S(2)}, u32[]{:S(2)}) collective-permute-start(bf16[8,8,1024]{2,1,0:T(8,128)(2,1)S(1)} %all-to-all-done.refs_4_), channel_id=1, source_target_pairs={{0,16},{8,24},{16,32},{24,40},{32,48},{40,56},{48,64},{56,72},{64,... | collective-permute-start | bytes 393224 | tf_op jit(solution)/shard_map/ppermute | solution.py:27
  91.4 6.0 %collective-permute-start.4 = (bf16[8,8,1024]{2,1,0:T(8,128)(2,1)S(1)}, bf16[8,8,1024]{2,1,0:T(8,128)(2,1)S(1)}, u32[]{:S(2)}, u32[]{:S(2)}) collective-permute-start(bf16[8,8,1024]{2,1,0:T(8,128)(2,1)S(1)} %all-to-all-done.refs_4_), channel_id=1, source_target_pairs={{0,248},{8,0},{16,8},{24,16},{32,24},{40,32},{48,40},{56,48},{64,5... | collective-permute-start | bytes 393224 | tf_op jit(solution)/shard_map/ppermute | solution.py:27

commit v6 on v5

--- a/solution.py
+++ b/solution.py
@@ -52,14 +52,15 @@
     sims_ref[...] = lax.dot_general(
         whole, rows_ref[...], (((1,), (1,)), ((), ())), preferred_element_type=jnp.float32
     ).reshape(sims_ref.shape)
+    codes = jnp.concatenate([pack[count:, :128][:1].astype(jnp.float32) for pack in packs], axis=0).T
     biases = []
     best = jnp.full((8, at), LOW, jnp.float32)
-    for k, pack in enumerate(packs):
-        code = pack[count:, :128].astype(jnp.float32).T[:, :1]
+    for k in range(len(packs)):
+        code = codes[:, k : k + 1]
         bias = jnp.sum(jnp.where(docs == code, bias_ref[...], 0.0), axis=1, keepdims=True)
         valid = code < float(bias_ref.shape[1])
         biases.append(jnp.where(valid, bias, -jnp.inf))
-        sim = jnp.where(valid, sims_ref[k], LOW)
+        sim = sims_ref[k] + jnp.where(valid, 0.0, LOW)
         best = jnp.maximum(best, jnp.max(sim.reshape(count // 8, 8, at), axis=0))
     best = jnp.max(best, axis=0, keepdims=True)
     total = jnp.zeros((8, at), jnp.float32)

time: 132 us -> 132 us (level)
  no operation moved by 1% of the time
where the time goes in v6:
time: 132 us
  starting transfers between devices  80.5 us (61%)
  blocking collectives  31.4 us (24%)
  waiting for transfers between devices  13.7 us (10%)
  Pallas kernels  2.96 us (2%)
  other arithmetic  1.74 us (1%)
    all_to_all x1, starting transfers between devices, shards(): lax.all_to_all(copies, 'ring', 0, 0, axis_index_groups=loops, tiled=True)  48.2 us
    all_to_all x1, blocking collectives, shards(): lax.all_to_all(stats, GROUP, 0, 0, axis_index_groups=columns, tiled=True)  31.4 us
    ppermute x5, starting transfers between devices, shifted(): lax.ppermute(value, axis, [(k, (k + by) % size) for k in range(size)])  21 us
    ppermute x2, starting transfers between devices, mirrored(): return lax.ppermute(value, 'row', [(k, k ^ mask) for k in range(size)])  11.2 us
    all_to_all x1, waiting for transfers between devices, shards(): lax.all_to_all(copies, 'ring', 0, 0, axis_index_groups=loops, tiled=True)  5.84 us
    ppermute x5, waiting for transfers between devices, shifted(): lax.ppermute(value, axis, [(k, (k + by) % size) for k in range(size)])  3.99 us
    ppermute x2, waiting for transfers between devices, mirrored(): return lax.ppermute(value, 'row', [(k, k ^ mask) for k in range(size)])  3.92 us
  transfers between devices with their start and end apart: 8, of which 4 were waited for; matrix products, arithmetic and copies ran while one was open for 0% of the time, Pallas kernels for 0%

profile of v6, /device:TPU:33, one launch (start us, length us, event | category | flops | bytes accessed | tf_op | source)
XLA Modules:
  0.0 131.8 jit_solution(8831451843103514418)
XLA Ops:
  0.6 0.0 copy-start
  0.6 0.7 fusion.3
  1.3 1.0 fusion.4
  2.3 4.1 %collective-permute-start = (bf16[136,1024]{1,0:T(8,128)(2,1)S(1)}, bf16[136,1024]{1,0:T(8,128)(2,1)S(1)}, u32[]{:S(2)}, u32[]{:S(2)}) collective-permute-start(bf16[136,1024]{1,0:T(8,128)(2,1)S(1)} %get-tuple-element.7), channel_id=1, source_target_pairs={{0,2},{2,0},{4,6},{6,4},{1,3},{3,1},{5,7},{7,5},{8,10},{10,8},{12,... | collective-permute-start | bytes 835592 | tf_op jit(solution)/shard_map/ppermute | solution.py:32
  6.5 3.9 %collective-permute-done = bf16[136,1024]{1,0:T(8,128)(2,1)S(1)} collective-permute-done((bf16[136,1024]{1,0:T(8,128)(2,1)S(1)}, bf16[136,1024]{1,0:T(8,128)(2,1)S(1)}, u32[]{:S(2)}, u32[]{:S(2)}) %collective-permute-start) | collective-permute-done | bytes 278560 | tf_op jit(solution)/shard_map/ppermute | solution.py:32
  10.4 0.1 pad_maximum_fusion.refs_0_
  10.4 7.1 %collective-permute-start.1 = (bf16[2,136,1024]{2,1,0:T(8,128)(2,1)S(1)}, bf16[2,136,1024]{2,1,0:T(8,128)(2,1)S(1)}, u32[]{:S(2)}, u32[]{:S(2)}) collective-permute-start(bf16[2,136,1024]{2,1,0:T(8,128)(2,1)S(1)} %pad_maximum_fusion.refs_0_), channel_id=1, source_target_pairs={{0,6},{2,4},{4,2},{6,0},{1,7},{3,5},{5,3},{7,1},{8,14},{10,12},{12... | collective-permute-start | bytes 1671176 | tf_op jit(solution)/shard_map/ppermute | solution.py:32
  17.6 0.0 copy-done
  17.6 0.6 broadcast_in_dim.23
  18.3 48.2 %all-to-all-start = ((bf16[8,8,1024]{2,1,0:T(8,128)(2,1)}), bf16[8,8,1024]{2,1,0:T(8,128)(2,1)S(1)}, u32[]{:S(2)}, u32[]{:S(2)}) async-start(bf16[8,8,1024]{2,1,0:T(8,128)(2,1)} %broadcast_in_dim.23), calls=%async_computation | async-start | bytes 262144 | tf_op jit(solution)/shard_map/all_to_all | solution.py:114
  66.5 4.2 %collective-permute-start.2 = (bf16[2,136,1024]{2,1,0:T(8,128)(2,1)S(1)}, bf16[2,136,1024]{2,1,0:T(8,128)(2,1)S(1)}, u32[]{:S(2)}, u32[]{:S(2)}) collective-permute-start(bf16[2,136,1024]{2,1,0:T(8,128)(2,1)S(1)} %pad_maximum_fusion.refs_0_), channel_id=1, source_target_pairs={{0,1},{1,0},{2,3},{3,2},{4,5},{5,4},{6,7},{7,6},{8,9},{9,8},{10,11... | collective-permute-start | bytes 1671176 | tf_op jit(solution)/shard_map/ppermute | solution.py:27
  70.7 0.0 collective-permute-done.1.refs_1_
  70.8 2.0 %collective-permute-start.3 = (bf16[2,136,1024]{2,1,0:T(8,128)(2,1)S(1)}, bf16[2,136,1024]{2,1,0:T(8,128)(2,1)S(1)}, u32[]{:S(2)}, u32[]{:S(2)}) collective-permute-start(bf16[2,136,1024]{2,1,0:T(8,128)(2,1)S(1)} %collective-permute-done.1.refs_1_), channel_id=1, source_target_pairs={{0,1},{1,0},{2,3},{3,2},{4,5},{5,4},{6,7},{7,6},{8,9},{9,8},{10,11... | collective-permute-start | bytes 1671176 | tf_op jit(solution)/shard_map/ppermute | solution.py:27
  72.7 5.8 %all-to-all-done.refs_4_ = bf16[8,8,1024]{2,1,0:T(8,128)(2,1)S(1)} async-done(((bf16[8,8,1024]{2,1,0:T(8,128)(2,1)}), bf16[8,8,1024]{2,1,0:T(8,128)(2,1)S(1)}, u32[]{:S(2)}, u32[]{:S(2)}) %all-to-all-start) | async-done | bytes 131104 | tf_op jit(solution)/shard_map/all_to_all | solution.py:114
  78.6 7.9 %collective-permute-start.6 = (bf16[8,8,1024]{2,1,0:T(8,128)(2,1)S(1)}, bf16[8,8,1024]{2,1,0:T(8,128)(2,1)S(1)}, u32[]{:S(2)}, u32[]{:S(2)}) collective-permute-start(bf16[8,8,1024]{2,1,0:T(8,128)(2,1)S(1)} %all-to-all-done.refs_4_), channel_id=1, source_target_pairs={{0,8},{8,16},{16,24},{24,32},{32,40},{40,48},{48,56},{56,64},{64,7... | collective-permute-start | bytes 393224 | tf_op jit(solution)/shard_map/ppermute | solution.py:27
  86.4 4.9 %collective-permute-start.5 = (bf16[8,8,1024]{2,1,0:T(8,128)(2,1)S(1)}, bf16[8,8,1024]{2,1,0:T(8,128)(2,1)S(1)}, u32[]{:S(2)}, u32[]{:S(2)}) collective-permute-start(bf16[8,8,1024]{2,1,0:T(8,128)(2,1)S(1)} %all-to-all-done.refs_4_), channel_id=1, source_target_pairs={{0,16},{8,24},{16,32},{24,40},{32,48},{40,56},{48,64},{56,72},{64,... | collective-permute-start | bytes 393224 | tf_op jit(solution)/shard_map/ppermute | solution.py:27
  91.4 2.0 %collective-permute-start.4 = (bf16[8,8,1024]{2,1,0:T(8,128)(2,1)S(1)}, bf16[8,8,1024]{2,1,0:T(8,128)(2,1)S(1)}, u32[]{:S(2)}, u32[]{:S(2)}) collective-permute-start(bf16[8,8,1024]{2,1,0:T(8,128)(2,1)S(1)} %all-to-all-done.refs_4_), channel_id=1, source_target_pairs={{0,248},{8,0},{16,8},{24,16},{32,24},{40,32},{48,40},{56,48},{64,5... | collective-permute-start | bytes 393224 | tf_op jit(solution)/shard_map/ppermute | solution.py:27
  93.4 0.0 collective-permute-done.2.refs_2_
  93.4 0.0 collective-permute-done.6.refs_7_
  93.4 2.9 %collective-permute-done.5.refs_6_ = bf16[8,8,1024]{2,1,0:T(8,128)(2,1)S(1)} collective-permute-done((bf16[8,8,1024]{2,1,0:T(8,128)(2,1)S(1)}, bf16[8,8,1024]{2,1,0:T(8,128)(2,1)S(1)}, u32[]{:S(2)}, u32[]{:S(2)}) %collective-permute-start.5) | collective-permute-done | bytes 131104 | tf_op jit(solution)/shard_map/ppermute | solution.py:27
  96.4 1.1 collective-permute-done.4.refs_5_
  97.4 0.0 collective-permute-done.3.refs_3_
  97.4 2.3 %scores.1 = f32[64,128]{1,0:T(8,128)S(1)} custom-call(s32[1]{0:T(128)} %bitcast.shift_ref, f32[1,128]{1,0:T(1,128)} %bitcast.16, bf16[2,136,1024]{2,1,0:T(8,128)(2,1)S(1)} %pad_maximum_fusion.refs_0_, bf16[2,136,1024]{2,1,0:T(8,128)(2,1)S(1)} %collective-permute-done.1.refs_1_, bf16[2,136,1024]{2,1,0:T(8,128)(2,1)S(1)} %collective-permute-done.2.refs_2_, ...), custom_call_target="tpu_custom_call" | custom-call | tf_op jit(solution)/shard_map/scores/pallas_call | solution.py:124
  99.7 31.4 %all_to_all.16 = f32[64,1,128]{2,1,0:T(1,128)S(1)} all-to-all(f32[64,1,128]{2,1,0:T(1,128)S(1)} %bitcast.13), channel_id=1, replica_groups={{128,160,192,224,0,32,64,96,136,168,200,232,8,40,72,104,144,176,208,240..., dimensions={0} | all-to-all | bytes 65536 | tf_op jit(solution)/shard_map/all_to_all | solution.py:148
  131.1 0.7 finish.1
  (1 shorter events, 0.0 us)
Async XLA Ops:
  0.6 16.9 %copy-start = (bf16[16,1024]{1,0:T(8,128)(2,1)S(1)}, bf16[16,1024]{1,0:T(8,128)(2,1)}, u32[]{:S(2)}) copy-start(bf16[16,1024]{1,0:T(8,128)(2,1)} %param.5) | copy-start | bytes 98308
  2.3 8.0 %collective-permute-start = (bf16[136,1024]{1,0:T(8,128)(2,1)S(1)}, bf16[136,1024]{1,0:T(8,128)(2,1)S(1)}, u32[]{:S(2)}, u32[]{:S(2)}) collective-permute-start(bf16[136,1024]{1,0:T(8,128)(2,1)S(1)} %get-tuple-element.7), channel_id=1, source_target_pairs={{0,2},{2,0},{4,6},{6,4},{1,3},{3,1},{5,7},{7,5},{8,10},{10,8},{12,... | collective-permute-start | bytes 835592 | tf_op jit(solution)/shard_map/ppermute | solution.py:32
  10.4 60.3 %collective-permute-start.1 = (bf16[2,136,1024]{2,1,0:T(8,128)(2,1)S(1)}, bf16[2,136,1024]{2,1,0:T(8,128)(2,1)S(1)}, u32[]{:S(2)}, u32[]{:S(2)}) collective-permute-start(bf16[2,136,1024]{2,1,0:T(8,128)(2,1)S(1)} %pad_maximum_fusion.refs_0_), channel_id=1, source_target_pairs={{0,6},{2,4},{4,2},{6,0},{1,7},{3,5},{5,3},{7,1},{8,14},{10,12},{12... | collective-permute-start | bytes 1671176 | tf_op jit(solution)/shard_map/ppermute | solution.py:32
  18.3 60.3 %all-to-all-start = ((bf16[8,8,1024]{2,1,0:T(8,128)(2,1)}), bf16[8,8,1024]{2,1,0:T(8,128)(2,1)S(1)}, u32[]{:S(2)}, u32[]{:S(2)}) async-start(bf16[8,8,1024]{2,1,0:T(8,128)(2,1)} %broadcast_in_dim.23), calls=%async_computation | async-start | bytes 262144 | tf_op jit(solution)/shard_map/all_to_all | solution.py:114
  66.5 26.9 %collective-permute-start.2 = (bf16[2,136,1024]{2,1,0:T(8,128)(2,1)S(1)}, bf16[2,136,1024]{2,1,0:T(8,128)(2,1)S(1)}, u32[]{:S(2)}, u32[]{:S(2)}) collective-permute-start(bf16[2,136,1024]{2,1,0:T(8,128)(2,1)S(1)} %pad_maximum_fusion.refs_0_), channel_id=1, source_target_pairs={{0,1},{1,0},{2,3},{3,2},{4,5},{5,4},{6,7},{7,6},{8,9},{9,8},{10,11... | collective-permute-start | bytes 1671176 | tf_op jit(solution)/shard_map/ppermute | solution.py:27
  70.8 26.7 %collective-permute-start.3 = (bf16[2,136,1024]{2,1,0:T(8,128)(2,1)S(1)}, bf16[2,136,1024]{2,1,0:T(8,128)(2,1)S(1)}, u32[]{:S(2)}, u32[]{:S(2)}) collective-permute-start(bf16[2,136,1024]{2,1,0:T(8,128)(2,1)S(1)} %collective-permute-done.1.refs_1_), channel_id=1, source_target_pairs={{0,1},{1,0},{2,3},{3,2},{4,5},{5,4},{6,7},{7,6},{8,9},{9,8},{10,11... | collective-permute-start | bytes 1671176 | tf_op jit(solution)/shard_map/ppermute | solution.py:27
  78.6 14.9 %collective-permute-start.6 = (bf16[8,8,1024]{2,1,0:T(8,128)(2,1)S(1)}, bf16[8,8,1024]{2,1,0:T(8,128)(2,1)S(1)}, u32[]{:S(2)}, u32[]{:S(2)}) collective-permute-start(bf16[8,8,1024]{2,1,0:T(8,128)(2,1)S(1)} %all-to-all-done.refs_4_), channel_id=1, source_target_pairs={{0,8},{8,16},{16,24},{24,32},{32,40},{40,48},{48,56},{56,64},{64,7... | collective-permute-start | bytes 393224 | tf_op jit(solution)/shard_map/ppermute | solution.py:27
  86.4 9.9 %collective-permute-start.5 = (bf16[8,8,1024]{2,1,0:T(8,128)(2,1)S(1)}, bf16[8,8,1024]{2,1,0:T(8,128)(2,1)S(1)}, u32[]{:S(2)}, u32[]{:S(2)}) collective-permute-start(bf16[8,8,1024]{2,1,0:T(8,128)(2,1)S(1)} %all-to-all-done.refs_4_), channel_id=1, source_target_pairs={{0,16},{8,24},{16,32},{24,40},{32,48},{40,56},{48,64},{56,72},{64,... | collective-permute-start | bytes 393224 | tf_op jit(solution)/shard_map/ppermute | solution.py:27
  91.4 6.0 %collective-permute-start.4 = (bf16[8,8,1024]{2,1,0:T(8,128)(2,1)S(1)}, bf16[8,8,1024]{2,1,0:T(8,128)(2,1)S(1)}, u32[]{:S(2)}, u32[]{:S(2)}) collective-permute-start(bf16[8,8,1024]{2,1,0:T(8,128)(2,1)S(1)} %all-to-all-done.refs_4_), channel_id=1, source_target_pairs={{0,248},{8,0},{16,8},{24,16},{32,24},{40,32},{48,40},{56,48},{64,5... | collective-permute-start | bytes 393224 | tf_op jit(solution)/shard_map/ppermute | solution.py:27
